TPU v7x, 256 devices: a whole 4x4x8 slice. The times are simulated.
256 devices in a mesh: seq: 32 (over y_lo, z, core), head: 8 (over x, y_hi).
Axes of the slice: x: 4, y: 4 (y_hi: 2, y_lo: 2; y = y_hi * 2 + y_lo), z: 8, core: 2. Of those that a mesh axis runs over, the one named last changes fastest.
Arguments:
- prefix_embed: bfloat16 [256, 1024], replicated, may hold values from -6 to 6
- w_hidden: bfloat16 [1024, 8192], P(None, 'seq'), may hold values from -0.1875 to 0.1875
- b_hidden: float32 [8192], P('seq'), may hold values from -4 to 4
- w_out: bfloat16 [8192, 2, 1024], P('seq', None, 'head'), may hold values from -0.0625 to 0.0625
- queries: bfloat16 [4096, 8192], P('seq', 'head'), may hold values from -6 to 6
- keys: bfloat16 [4096, 1024], P('seq', 'head'), may hold values from -6 to 6
- values: bfloat16 [4096, 1024], P('seq', 'head'), may hold values from -6 to 6
- out_grad: bfloat16 [4096, 8192], P('seq', 'head'), may hold values from -6 to 6
Outputs:
- query_grad: bfloat16 [4096, 8192], P('seq', 'head')
- grad_w_out: float32 [8192, 2, 1024], P('seq', None, 'head')
- grad_w_hidden: float32 [1024, 8192], P(None, 'seq')
- grad_b_hidden: float32 [8192], P('seq')
- grad_prefix: float32 [256, 1024], replicated
All inputs are finite; a program needn't handle non-finite values.
Results may differ from a plain program's by a relative error of at most 0.008.
Values may be sent and summed in bfloat16 or wider, within the bound.
No kernel may reach another device: no remote copies, remote signals or barrier semaphores. Data moves between devices by JAX's collectives and lax.ppermute only.
A program may use at most 64 MiB of HBM per device.

v0:
```python
import math

import jax
import jax.numpy as jnp
from jax import lax
from jax.sharding import Mesh
from jax.sharding import PartitionSpec as P

QH = 64
KVH = 8
HD = 128
SEQ = ("seq_0", "seq_1", "seq_2")


def padded_to(lines, count):
    spare = -lines.shape[0] % count
    if not spare:
        return lines
    return jnp.concatenate([lines, jnp.zeros((spare, *lines.shape[1:]), lines.dtype)])


def from_everyone(value, axis):
    copies = jnp.broadcast_to(value, (lax.axis_size(axis), *value.shape))
    return lax.all_to_all(copies, axis, split_axis=0, concat_axis=0, tiled=True)


def laid_out(parts, dim):
    parts = jnp.moveaxis(parts, 0, dim)
    lengths = parts.shape
    return parts.reshape(*lengths[:dim], lengths[dim] * lengths[dim + 1], *lengths[dim + 2 :])


def collect(value, axis, dim):
    parts = from_everyone(value, axis)
    return laid_out(parts, dim)


def in_blocks(value, dim, count):
    before, after = (value.shape[:dim], value.shape[dim + 1 :])
    return jnp.moveaxis(value.reshape(*before, count, -1, *after), dim, 0)


def sum_at_owner(value, axis, dim):
    count = lax.axis_size(axis)
    parts = lax.all_to_all(in_blocks(value, dim, count), axis, 0, 0, tiled=True)
    return jnp.sum(parts, axis=0)


def sum_by_parts(value, axes):
    lines = value.reshape(-1, value.shape[-1])
    padded = padded_to(lines, lax.axis_size(axes))
    whole = collect(sum_at_owner(padded, axes, 0), axes, 0)
    return lax.slice_in_dim(whole, 0, len(lines)).reshape(value.shape)


def shifted(value, axis, steps):
    count = lax.axis_size(axis)
    first, last = (max(0, -steps), min(count, count - steps))
    return lax.ppermute(value, axis, [(source, source + steps) for source in range(first, last)])


def of_everyone(value, axis):
    everything = from_everyone(value, axis)
    return jnp.sum(everything, axis=0)


def sum_by_axis(value, axes, dim):
    far, near = axes
    own = sum_at_owner(in_blocks(value, dim, lax.axis_size(far)), near, dim + 1)
    return jnp.sum(lax.all_to_all(own, far, 0, 0, tiled=True), axis=0)


def whole_of(value, axes, dim):
    far, near = axes
    first = from_everyone(value, far)
    parts = jnp.swapaxes(from_everyone(first, near), 0, 1)
    return laid_out(parts.reshape(-1, *value.shape), dim)


def sum_by_parts_2(value, axes):
    lines = value.reshape(-1, value.shape[-1])
    own = sum_by_axis(padded_to(lines, lax.axis_size(axes[0]) * lax.axis_size(axes[1])), axes, 0)
    whole = whole_of(own, axes, 0)
    return whole[: len(lines)].reshape(value.shape)


def key_sweep(running, key_part, value_part, offset, bounds, update):
    seq_start, last_pos = bounds
    key_count = key_part.shape[0]
    block_len = math.gcd(key_count, 512)
    heads_here = key_part.shape[1] // HD

    def advance(turn, held):
        first_key = offset + turn * block_len
        key_block = lax.dynamic_slice_in_dim(key_part, turn * block_len, block_len, 0).reshape(
            block_len, heads_here, HD
        )
        value_block = lax.dynamic_slice_in_dim(value_part, turn * block_len, block_len, 0).reshape(
            block_len, heads_here, HD
        )
        useful = (first_key <= last_pos) & (first_key + block_len - 1 >= seq_start)
        return lax.cond(
            useful,
            lambda kept: update(kept, key_block, value_block, first_key),
            lambda kept: kept,
            held,
        )

    return lax.fori_loop(0, key_count // block_len, advance, running)


def on_device(prefix_embed, w_hidden, b_hidden, w_out, queries, keys, values, out_grad):
    scaling = 1.0 / math.sqrt(HD)
    group = QH // KVH
    hidden_pre = jnp.dot(prefix_embed, w_hidden, preferred_element_type=jnp.float32) + b_hidden
    tangent = jnp.tanh(hidden_pre)
    hidden = tangent.astype(jnp.bfloat16)
    partial_kv = jnp.einsum("ph,hck->pck", hidden, w_out, preferred_element_type=jnp.float32)
    prefix_kv = sum_by_parts(partial_kv, SEQ).astype(jnp.bfloat16)
    tok_count = queries.shape[0]
    span = lax.axis_size(SEQ)
    seq_length = tok_count * span
    heads_here = keys.shape[1] // HD
    prefix_len = prefix_kv.shape[0]
    prefix_keys = prefix_kv[:, 0].reshape(prefix_len, heads_here, HD)
    prefix_values = prefix_kv[:, 1].reshape(prefix_len, heads_here, HD)

    def by_head(rows):
        return (
            rows.reshape(tok_count, heads_here, group, HD)
            .transpose(1, 0, 2, 3)
            .reshape(heads_here, tok_count * group, HD)
        )

    query_rows = by_head(queries)
    grad_rows = by_head(out_grad)
    my_start = lax.axis_index(SEQ) * tok_count
    last_pos = my_start + tok_count - 1
    seq_start = my_start // seq_length * seq_length
    bounds = (seq_start, last_pos)
    query_pos = my_start + jnp.arange(tok_count * group, dtype=jnp.int32) // group
    local_pair = jnp.stack([keys, values], 0)

    def block_scores(key_block, value_block, first_key):
        logits = (
            jnp.einsum("grd,ngd->grn", query_rows, key_block, preferred_element_type=jnp.float32)
            * scaling
        )
        dot_grads = jnp.einsum(
            "grd,ngd->grn", grad_rows, value_block, preferred_element_type=jnp.float32
        )
        key_pos = first_key + jnp.arange(key_block.shape[0], dtype=jnp.int32)
        seen = (key_pos[None, None, :] <= query_pos[None, :, None]) & (
            key_pos[None, None, :] >= seq_start
        )
        logits = jnp.where(seen, logits, -1e30)
        return (logits, dot_grads)

    def forward_update(running, key_block, value_block, first_key):
        run_max, run_sum, run_dot = running
        logits, dot_grads = block_scores(key_block, value_block, first_key)
        new_max = jnp.maximum(run_max, jnp.max(logits, axis=-1))
        rescale = jnp.exp(run_max - new_max)
        weights = jnp.exp(logits - new_max[..., None])
        return (
            new_max,
            run_sum * rescale + jnp.sum(weights, axis=-1),
            run_dot * rescale + jnp.sum(weights * dot_grads, axis=-1),
        )

    prefix_logits = (
        jnp.einsum("grd,ngd->grn", query_rows, prefix_keys, preferred_element_type=jnp.float32)
        * scaling
    )
    prefix_dots = jnp.einsum(
        "grd,ngd->grn", grad_rows, prefix_values, preferred_element_type=jnp.float32
    )
    start_max = jnp.max(prefix_logits, axis=-1)
    start_weights = jnp.exp(prefix_logits - start_max[..., None])
    start_state = (
        start_max,
        jnp.sum(start_weights, axis=-1),
        jnp.sum(start_weights * prefix_dots, axis=-1),
    )
    start_state = key_sweep(start_state, keys, values, my_start, bounds, forward_update)
    held_empty = jnp.zeros((span,) + local_pair.shape, local_pair.dtype)
    held_empty = held_empty.at[span - 1].set(local_pair)

    def collect_turn(turn, carry):
        held, piece = carry
        moved = shifted(piece, SEQ, 1)
        held = lax.dynamic_update_index_in_dim(held, moved, span - 2 - turn, 0)
        return (held, moved)

    held, unused = lax.fori_loop(0, span - 1, collect_turn, (held_empty, local_pair))
    earlier = held[: span - 1]
    key_all = earlier[:, 0].reshape((span - 1) * tok_count, keys.shape[1])
    value_all = earlier[:, 1].reshape((span - 1) * tok_count, keys.shape[1])
    earliest = my_start - (span - 1) * tok_count
    final_state = key_sweep(start_state, key_all, value_all, earliest, bounds, forward_update)
    run_max, run_sum, run_dot = final_state
    log_total = run_max + jnp.log(run_sum)
    delta_row = run_dot / run_sum

    def backward_update(total, key_block, value_block, first_key):
        logits, dot_grads = block_scores(key_block, value_block, first_key)
        probs = jnp.exp(logits - log_total[..., None])
        score_grad = (probs * (dot_grads - delta_row[..., None])).astype(jnp.bfloat16)
        return total + jnp.einsum(
            "grn,ngd->grd", score_grad, key_block, preferred_element_type=jnp.float32
        )

    prefix_probs = jnp.exp(prefix_logits - log_total[..., None])
    prefix_score_grad = (prefix_probs * (prefix_dots - delta_row[..., None])).astype(jnp.bfloat16)
    start_total = jnp.einsum(
        "grn,ngd->grd", prefix_score_grad, prefix_keys, preferred_element_type=jnp.float32
    )
    start_total = key_sweep(start_total, keys, values, my_start, bounds, backward_update)
    total = key_sweep(start_total, key_all, value_all, earliest, bounds, backward_update)
    query_grad = (total * scaling).reshape(heads_here, tok_count, group, HD).transpose(1, 0, 2, 3)
    query_grad = query_grad.reshape(tok_count, heads_here * group * HD).astype(jnp.bfloat16)
    key_grad = (
        jnp.einsum(
            "grn,grd->ngd", prefix_score_grad, query_rows, preferred_element_type=jnp.float32
        )
        * scaling
    )
    value_grad = jnp.einsum(
        "grn,grd->ngd",
        prefix_probs.astype(jnp.bfloat16),
        grad_rows,
        preferred_element_type=jnp.float32,
    )
    both_grads = jnp.stack(
        [
            key_grad.reshape(prefix_len, heads_here * HD),
            value_grad.reshape(prefix_len, heads_here * HD),
        ],
        1,
    )
    prefix_grads = sum_by_parts(both_grads, SEQ).astype(jnp.bfloat16)
    grad_w_out = jnp.einsum("ph,pck->hck", hidden, prefix_grads, preferred_element_type=jnp.float32)
    hidden_part = jnp.einsum("pck,hck->ph", prefix_grads, w_out, preferred_element_type=jnp.float32)
    hidden_grad = of_everyone(hidden_part, "head")
    pre_grad = hidden_grad * (1.0 - tangent * tangent)
    pre_rounded = pre_grad.astype(jnp.bfloat16)
    grad_w_hidden = lax.dot_general(
        prefix_embed, pre_rounded, (((0,), (0,)), ((), ())), preferred_element_type=jnp.float32
    )
    grad_b_hidden = jnp.sum(pre_grad, axis=0)
    embed_part = lax.dot_general(
        pre_rounded, w_hidden, (((1,), (1,)), ((), ())), preferred_element_type=jnp.float32
    )
    grad_prefix = sum_by_parts_2(embed_part, (("seq_0", "seq_1"), "seq_2"))
    return (query_grad, grad_w_out, grad_w_hidden, grad_b_hidden, grad_prefix)


def solution(mesh):
    torus = Mesh(
        mesh.devices.reshape(2, 8, 2, mesh.shape["head"]), ("seq_0", "seq_1", "seq_2", "head")
    )
    placed = (
        P(),
        P(None, SEQ),
        P(SEQ),
        P(SEQ, None, "head"),
        P(SEQ, "head"),
        P(SEQ, "head"),
        P(SEQ, "head"),
        P(SEQ, "head"),
    )
    return jax.shard_map(
        on_device,
        mesh=torus,
        in_specs=placed,
        out_specs=(P(SEQ, "head"), P(SEQ, None, "head"), P(None, SEQ), P(SEQ), P()),
        check_vma=False,
    )
```

profile of v0, /device:TPU:233, one launch (start us, length us, event | category | flops | bytes accessed | tf_op | source)
XLA Modules:
  0.0 530.2 jit_solution(2336397823795167744)
XLA Ops:
  5.1 7.3 %all-to-all-start = ((f32[32,16,128]{2,1,0:T(8,128)}), f32[32,16,128]{2,1,0:T(8,128)}, u32[]{:S(2)}, u32[]{:S(2)}) async-start(f32[32,16,128]{2,1,0:T(8,128)} %bitcast.32), calls=%async_computation | async-start | bytes 524288 | tf_op jit(solution)/shard_map/all_to_all | solution.py:45
  15.5 5.1 all-to-all-done
  22.2 9.6 %all-to-all-start.1 = ((bf16[32,16,128]{2,1,0:T(8,128)(2,1)}), bf16[32,16,128]{2,1,0:T(8,128)(2,1)}, u32[]{:S(2)}, u32[]{:S(2)}) async-start(bf16[32,16,128]{2,1,0:T(8,128)(2,1)} %broadcast_in_dim.49), calls=%async_computation.1 | async-start | bytes 262144 | tf_op jit(solution)/shard_map/all_to_all | solution.py:24
  31.8 217.2 %while.73 = (s32[]{:T(128)}, bf16[32,2,128,128]{3,2,1,0:T(8,128)(2,1)S(1)}, bf16[2,128,128]{2,1,0:T(8,128)(2,1)}, s32[]{:T(128)}, s32[]{:T(128)}, /*index=5*/s32[]{:T(128)}, s32[]{:T(128)}) while((s32[]{:T(128)}, bf16[32,2,128,128]{3,2,1,0:T(8,128)(2,1)S(1)}, bf16[2,128,128]{2,1,0:T(8,128)(2,1)}, s32[]{:T(128)}, s32[]{:T(128)}, ...), condition=%wide.region_10.11_spmd, body=%wide.region_9.10_spmd.sunk | while | flops 6 | bytes 524455 | solution.py:195
  37.1 4.7 collective-permute-done
  43.8 4.5 collective-permute-done
  121.3 4.5 collective-permute-done
  127.7 5.7 %collective-permute-done = bf16[2,128,128]{2,1,0:T(8,128)(2,1)S(1)} collective-permute-done((bf16[2,128,128]{2,1,0:T(8,128)(2,1)}, bf16[2,128,128]{2,1,0:T(8,128)(2,1)S(1)}, u32[]{:S(2)}, u32[]{:S(2)}) %collective-permute-start) | collective-permute-done | bytes 65568 | tf_op jit(solution)/shard_map/while/body/eval_jaxpr/ppermute | solution.py:59
  135.4 5.7 %collective-permute-done = bf16[2,128,128]{2,1,0:T(8,128)(2,1)S(1)} collective-permute-done((bf16[2,128,128]{2,1,0:T(8,128)(2,1)}, bf16[2,128,128]{2,1,0:T(8,128)(2,1)S(1)}, u32[]{:S(2)}, u32[]{:S(2)}) %collective-permute-start) | collective-permute-done | bytes 65568 | tf_op jit(solution)/shard_map/while/body/eval_jaxpr/ppermute | solution.py:59
  143.1 5.7 %collective-permute-done = bf16[2,128,128]{2,1,0:T(8,128)(2,1)S(1)} collective-permute-done((bf16[2,128,128]{2,1,0:T(8,128)(2,1)}, bf16[2,128,128]{2,1,0:T(8,128)(2,1)S(1)}, u32[]{:S(2)}, u32[]{:S(2)}) %collective-permute-start) | collective-permute-done | bytes 65568 | tf_op jit(solution)/shard_map/while/body/eval_jaxpr/ppermute | solution.py:59
  150.7 5.7 %collective-permute-done = bf16[2,128,128]{2,1,0:T(8,128)(2,1)S(1)} collective-permute-done((bf16[2,128,128]{2,1,0:T(8,128)(2,1)}, bf16[2,128,128]{2,1,0:T(8,128)(2,1)S(1)}, u32[]{:S(2)}, u32[]{:S(2)}) %collective-permute-start) | collective-permute-done | bytes 65568 | tf_op jit(solution)/shard_map/while/body/eval_jaxpr/ppermute | solution.py:59
  158.4 5.7 %collective-permute-done = bf16[2,128,128]{2,1,0:T(8,128)(2,1)S(1)} collective-permute-done((bf16[2,128,128]{2,1,0:T(8,128)(2,1)}, bf16[2,128,128]{2,1,0:T(8,128)(2,1)S(1)}, u32[]{:S(2)}, u32[]{:S(2)}) %collective-permute-start) | collective-permute-done | bytes 65568 | tf_op jit(solution)/shard_map/while/body/eval_jaxpr/ppermute | solution.py:59
  166.0 5.7 %collective-permute-done = bf16[2,128,128]{2,1,0:T(8,128)(2,1)S(1)} collective-permute-done((bf16[2,128,128]{2,1,0:T(8,128)(2,1)}, bf16[2,128,128]{2,1,0:T(8,128)(2,1)S(1)}, u32[]{:S(2)}, u32[]{:S(2)}) %collective-permute-start) | collective-permute-done | bytes 65568 | tf_op jit(solution)/shard_map/while/body/eval_jaxpr/ppermute | solution.py:59
  173.7 5.7 %collective-permute-done = bf16[2,128,128]{2,1,0:T(8,128)(2,1)S(1)} collective-permute-done((bf16[2,128,128]{2,1,0:T(8,128)(2,1)}, bf16[2,128,128]{2,1,0:T(8,128)(2,1)S(1)}, u32[]{:S(2)}, u32[]{:S(2)}) %collective-permute-start) | collective-permute-done | bytes 65568 | tf_op jit(solution)/shard_map/while/body/eval_jaxpr/ppermute | solution.py:59
  181.4 5.7 %collective-permute-done = bf16[2,128,128]{2,1,0:T(8,128)(2,1)S(1)} collective-permute-done((bf16[2,128,128]{2,1,0:T(8,128)(2,1)}, bf16[2,128,128]{2,1,0:T(8,128)(2,1)S(1)}, u32[]{:S(2)}, u32[]{:S(2)}) %collective-permute-start) | collective-permute-done | bytes 65568 | tf_op jit(solution)/shard_map/while/body/eval_jaxpr/ppermute | solution.py:59
  189.0 5.7 %collective-permute-done = bf16[2,128,128]{2,1,0:T(8,128)(2,1)S(1)} collective-permute-done((bf16[2,128,128]{2,1,0:T(8,128)(2,1)}, bf16[2,128,128]{2,1,0:T(8,128)(2,1)S(1)}, u32[]{:S(2)}, u32[]{:S(2)}) %collective-permute-start) | collective-permute-done | bytes 65568 | tf_op jit(solution)/shard_map/while/body/eval_jaxpr/ppermute | solution.py:59
  196.7 5.7 %collective-permute-done = bf16[2,128,128]{2,1,0:T(8,128)(2,1)S(1)} collective-permute-done((bf16[2,128,128]{2,1,0:T(8,128)(2,1)}, bf16[2,128,128]{2,1,0:T(8,128)(2,1)S(1)}, u32[]{:S(2)}, u32[]{:S(2)}) %collective-permute-start) | collective-permute-done | bytes 65568 | tf_op jit(solution)/shard_map/while/body/eval_jaxpr/ppermute | solution.py:59
  204.4 5.7 %collective-permute-done = bf16[2,128,128]{2,1,0:T(8,128)(2,1)S(1)} collective-permute-done((bf16[2,128,128]{2,1,0:T(8,128)(2,1)}, bf16[2,128,128]{2,1,0:T(8,128)(2,1)S(1)}, u32[]{:S(2)}, u32[]{:S(2)}) %collective-permute-start) | collective-permute-done | bytes 65568 | tf_op jit(solution)/shard_map/while/body/eval_jaxpr/ppermute | solution.py:59
  212.0 5.7 %collective-permute-done = bf16[2,128,128]{2,1,0:T(8,128)(2,1)S(1)} collective-permute-done((bf16[2,128,128]{2,1,0:T(8,128)(2,1)}, bf16[2,128,128]{2,1,0:T(8,128)(2,1)S(1)}, u32[]{:S(2)}, u32[]{:S(2)}) %collective-permute-start) | collective-permute-done | bytes 65568 | tf_op jit(solution)/shard_map/while/body/eval_jaxpr/ppermute | solution.py:59
  219.7 5.7 %collective-permute-done = bf16[2,128,128]{2,1,0:T(8,128)(2,1)S(1)} collective-permute-done((bf16[2,128,128]{2,1,0:T(8,128)(2,1)}, bf16[2,128,128]{2,1,0:T(8,128)(2,1)S(1)}, u32[]{:S(2)}, u32[]{:S(2)}) %collective-permute-start) | collective-permute-done | bytes 65568 | tf_op jit(solution)/shard_map/while/body/eval_jaxpr/ppermute | solution.py:59
  227.4 5.7 %collective-permute-done = bf16[2,128,128]{2,1,0:T(8,128)(2,1)S(1)} collective-permute-done((bf16[2,128,128]{2,1,0:T(8,128)(2,1)}, bf16[2,128,128]{2,1,0:T(8,128)(2,1)S(1)}, u32[]{:S(2)}, u32[]{:S(2)}) %collective-permute-start) | collective-permute-done | bytes 65568 | tf_op jit(solution)/shard_map/while/body/eval_jaxpr/ppermute | solution.py:59
  235.0 5.7 %collective-permute-done = bf16[2,128,128]{2,1,0:T(8,128)(2,1)S(1)} collective-permute-done((bf16[2,128,128]{2,1,0:T(8,128)(2,1)}, bf16[2,128,128]{2,1,0:T(8,128)(2,1)S(1)}, u32[]{:S(2)}, u32[]{:S(2)}) %collective-permute-start) | collective-permute-done | bytes 65568 | tf_op jit(solution)/shard_map/while/body/eval_jaxpr/ppermute | solution.py:59
  242.7 5.7 %collective-permute-done = bf16[2,128,128]{2,1,0:T(8,128)(2,1)S(1)} collective-permute-done((bf16[2,128,128]{2,1,0:T(8,128)(2,1)}, bf16[2,128,128]{2,1,0:T(8,128)(2,1)S(1)}, u32[]{:S(2)}, u32[]{:S(2)}) %collective-permute-start) | collective-permute-done | bytes 65568 | tf_op jit(solution)/shard_map/while/body/eval_jaxpr/ppermute | solution.py:59
  255.0 72.1 %while.74 = (s32[]{:T(128)}, f32[1,1024]{1,0:T(1,128)S(1)}, f32[1,1024]{1,0:T(1,128)S(1)}, f32[1,1024]{1,0:T(1,128)S(1)}, s32[]{:T(128)}, /*index=5*/s32[]{:T(12...) while((s32[]{:T(128)}, f32[1,1024]{1,0:T(1,128)S(1)}, ...), condition=%wide.region_17.18_spmd.clone, body=%wide.region_11.0_spmd.clone.sunk | while | flops 68432264 | bytes 2270913 | solution.py:109
  330.0 26.0 %all_to_all.45 = f32[32,16,128]{2,1,0:T(8,128)S(1)} all-to-all(f32[32,16,128]{2,1,0:T(8,128)S(1)} %bitcast.191), channel_id=1, replica_groups=mesh['seq_0'=2,'seq_1'=8,'seq_2'=2,'head'=8] {'seq_0','seq_1','seq_2'}, dimensions={0} | all-to-all | bytes 524288 | tf_op jit(solution)/shard_map/all_to_all | solution.py:45
  356.0 14.4 %all_to_all.46 = bf16[32,16,128]{2,1,0:T(8,128)(2,1)S(1)} all-to-all(bf16[32,16,128]{2,1,0:T(8,128)(2,1)S(1)} %broadcast_in_dim.60), channel_id=1, replica_groups=mesh['seq_0'=2,'seq_1'=8,'seq_2'=2,'head'=8] {'seq_0','seq_1','seq_2'}, dimensions={0} | all-to-all | bytes 262144 | tf_op jit(solution)/shard_map/all_to_all | solution.py:24
  370.8 33.4 %all_to_all.47 = f32[8,256,256]{2,1,0:T(8,128)S(1)} all-to-all(f32[8,256,256]{2,1,0:T(8,128)S(1)} %broadcast_in_dim.61), channel_id=1, replica_groups=mesh['seq_0'=2,'seq_1'=8,'seq_2'=2,'head'=8] {'head'}, dimensions={0} | all-to-all | bytes 4194304 | tf_op jit(solution)/shard_map/all_to_all | solution.py:24
  407.4 5.5 %all_to_all.48 = f32[2,16,8,1024]{3,2,1,0:T(8,128)S(1)} all-to-all(f32[2,16,8,1024]{3,2,1,0:T(8,128)S(1)} %bitcast.182), channel_id=1, replica_groups=mesh['seq_0'=2,'seq_1'=8,'seq_2'=2,'head'=8] {'seq_2'}, dimensions={0} | all-to-all | bytes 2097152 | tf_op jit(solution)/shard_map/all_to_all | solution.py:45
  413.8 6.7 %all-to-all-start.6 = ((f32[16,8,1024]{2,1,0:T(8,128)}), f32[16,8,1024]{2,1,0:T(8,128)S(1)}, u32[]{:S(2)}, u32[]{:S(2)}) async-start(f32[16,8,1024]{2,1,0:T(8,128)} %reduce_sum.128), calls=%async_computation.6 | async-start | bytes 1048576 | tf_op jit(solution)/shard_map/all_to_all | solution.py:70
  421.7 12.3 %all-to-all-done.6 = f32[16,8,1024]{2,1,0:T(8,128)S(1)} async-done(((f32[16,8,1024]{2,1,0:T(8,128)}), f32[16,8,1024]{2,1,0:T(8,128)S(1)}, u32[]{:S(2)}, u32[]{:S(2)}) %all-to-all-start.6) | async-done | bytes 524320 | tf_op jit(solution)/shard_map/all_to_all | solution.py:70
  434.9 6.9 %all-to-all-start.7 = ((f32[16,8,1024]{2,1,0:T(8,128)}), f32[16,8,1024]{2,1,0:T(8,128)S(1)}, u32[]{:S(2)}, u32[]{:S(2)}) async-start(f32[16,8,1024]{2,1,0:T(8,128)} %broadcast_in_dim.62), calls=%async_computation.7 | async-start | bytes 1048576 | tf_op jit(solution)/shard_map/all_to_all | solution.py:24
  441.8 78.4 %while.75 = (s32[]{:T(128)}, f32[1,1024,128]{2,1,0:T(8,128)S(1)}, s32[]{:T(128)}, s32[]{:T(128)}, s32[]{:T(128)}, /*index=5*/bf16[3968,128]{1,0:T(8,128)(2,1)}, ...) while((s32[]{:T(128)}, f32[1,1024,128]{2,1,0:T(8,128)S(1)}, ...), condition=%wide.region_23.24_spmd.clone, body=%wide.region_20.23_spmd.clone.sunk | while | flops 101852552 | bytes 2763405 | solution.py:109
  (814 shorter events, 436.1 us)
Async XLA Ops:
  5.1 15.5 %all-to-all-start = ((f32[32,16,128]{2,1,0:T(8,128)}), f32[32,16,128]{2,1,0:T(8,128)}, u32[]{:S(2)}, u32[]{:S(2)}) async-start(f32[32,16,128]{2,1,0:T(8,128)} %bitcast.32), calls=%async_computation | async-start | bytes 524288 | tf_op jit(solution)/shard_map/all_to_all | solution.py:45
  22.2 228.2 %all-to-all-start.1 = ((bf16[32,16,128]{2,1,0:T(8,128)(2,1)}), bf16[32,16,128]{2,1,0:T(8,128)(2,1)}, u32[]{:S(2)}, u32[]{:S(2)}) async-start(bf16[32,16,128]{2,1,0:T(8,128)(2,1)} %broadcast_in_dim.49), calls=%async_computation.1 | async-start | bytes 262144 | tf_op jit(solution)/shard_map/all_to_all | solution.py:24
  35.8 6.0 %collective-permute-start = (bf16[2,128,128]{2,1,0:T(8,128)(2,1)}, bf16[2,128,128]{2,1,0:T(8,128)(2,1)S(1)}, u32[]{:S(2)}, u32[]{:S(2)}) collective-permute-start(bf16[2,128,128]{2,1,0:T(8,128)(2,1)} %get-tuple-element.1740), channel_id=1, source_target_pairs={{0,8},{8,16},{16,24},{24,32},{32,40},{40,48},{48,56},{56,64},{64,7... | collective-permute-start | bytes 196616 | tf_op jit(solution)/shard_map/while/body/eval_jaxpr/ppermute | solution.py:59
  42.5 5.8 %collective-permute-start = (bf16[2,128,128]{2,1,0:T(8,128)(2,1)}, bf16[2,128,128]{2,1,0:T(8,128)(2,1)S(1)}, u32[]{:S(2)}, u32[]{:S(2)}) collective-permute-start(bf16[2,128,128]{2,1,0:T(8,128)(2,1)} %get-tuple-element.1740), channel_id=1, source_target_pairs={{0,8},{8,16},{16,24},{24,32},{32,40},{40,48},{48,56},{56,64},{64,7... | collective-permute-start | bytes 196616 | tf_op jit(solution)/shard_map/while/body/eval_jaxpr/ppermute | solution.py:59
  49.0 5.8 %collective-permute-start = (bf16[2,128,128]{2,1,0:T(8,128)(2,1)}, bf16[2,128,128]{2,1,0:T(8,128)(2,1)S(1)}, u32[]{:S(2)}, u32[]{:S(2)}) collective-permute-start(bf16[2,128,128]{2,1,0:T(8,128)(2,1)} %get-tuple-element.1740), channel_id=1, source_target_pairs={{0,8},{8,16},{16,24},{24,32},{32,40},{40,48},{48,56},{56,64},{64,7... | collective-permute-start | bytes 196616 | tf_op jit(solution)/shard_map/while/body/eval_jaxpr/ppermute | solution.py:59
  55.4 5.8 %collective-permute-start = (bf16[2,128,128]{2,1,0:T(8,128)(2,1)}, bf16[2,128,128]{2,1,0:T(8,128)(2,1)S(1)}, u32[]{:S(2)}, u32[]{:S(2)}) collective-permute-start(bf16[2,128,128]{2,1,0:T(8,128)(2,1)} %get-tuple-element.1740), channel_id=1, source_target_pairs={{0,8},{8,16},{16,24},{24,32},{32,40},{40,48},{48,56},{56,64},{64,7... | collective-permute-start | bytes 196616 | tf_op jit(solution)/shard_map/while/body/eval_jaxpr/ppermute | solution.py:59
  68.3 5.8 %collective-permute-start = (bf16[2,128,128]{2,1,0:T(8,128)(2,1)}, bf16[2,128,128]{2,1,0:T(8,128)(2,1)S(1)}, u32[]{:S(2)}, u32[]{:S(2)}) collective-permute-start(bf16[2,128,128]{2,1,0:T(8,128)(2,1)} %get-tuple-element.1740), channel_id=1, source_target_pairs={{0,8},{8,16},{16,24},{24,32},{32,40},{40,48},{48,56},{56,64},{64,7... | collective-permute-start | bytes 196616 | tf_op jit(solution)/shard_map/while/body/eval_jaxpr/ppermute | solution.py:59
  74.8 5.8 %collective-permute-start = (bf16[2,128,128]{2,1,0:T(8,128)(2,1)}, bf16[2,128,128]{2,1,0:T(8,128)(2,1)S(1)}, u32[]{:S(2)}, u32[]{:S(2)}) collective-permute-start(bf16[2,128,128]{2,1,0:T(8,128)(2,1)} %get-tuple-element.1740), channel_id=1, source_target_pairs={{0,8},{8,16},{16,24},{24,32},{32,40},{40,48},{48,56},{56,64},{64,7... | collective-permute-start | bytes 196616 | tf_op jit(solution)/shard_map/while/body/eval_jaxpr/ppermute | solution.py:59
  81.2 5.8 %collective-permute-start = (bf16[2,128,128]{2,1,0:T(8,128)(2,1)}, bf16[2,128,128]{2,1,0:T(8,128)(2,1)S(1)}, u32[]{:S(2)}, u32[]{:S(2)}) collective-permute-start(bf16[2,128,128]{2,1,0:T(8,128)(2,1)} %get-tuple-element.1740), channel_id=1, source_target_pairs={{0,8},{8,16},{16,24},{24,32},{32,40},{40,48},{48,56},{56,64},{64,7... | collective-permute-start | bytes 196616 | tf_op jit(solution)/shard_map/while/body/eval_jaxpr/ppermute | solution.py:59
  87.7 5.8 %collective-permute-start = (bf16[2,128,128]{2,1,0:T(8,128)(2,1)}, bf16[2,128,128]{2,1,0:T(8,128)(2,1)S(1)}, u32[]{:S(2)}, u32[]{:S(2)}) collective-permute-start(bf16[2,128,128]{2,1,0:T(8,128)(2,1)} %get-tuple-element.1740), channel_id=1, source_target_pairs={{0,8},{8,16},{16,24},{24,32},{32,40},{40,48},{48,56},{56,64},{64,7... | collective-permute-start | bytes 196616 | tf_op jit(solution)/shard_map/while/body/eval_jaxpr/ppermute | solution.py:59
  94.1 5.8 %collective-permute-start = (bf16[2,128,128]{2,1,0:T(8,128)(2,1)}, bf16[2,128,128]{2,1,0:T(8,128)(2,1)S(1)}, u32[]{:S(2)}, u32[]{:S(2)}) collective-permute-start(bf16[2,128,128]{2,1,0:T(8,128)(2,1)} %get-tuple-element.1740), channel_id=1, source_target_pairs={{0,8},{8,16},{16,24},{24,32},{32,40},{40,48},{48,56},{56,64},{64,7... | collective-permute-start | bytes 196616 | tf_op jit(solution)/shard_map/while/body/eval_jaxpr/ppermute | solution.py:59
  100.6 5.8 %collective-permute-start = (bf16[2,128,128]{2,1,0:T(8,128)(2,1)}, bf16[2,128,128]{2,1,0:T(8,128)(2,1)S(1)}, u32[]{:S(2)}, u32[]{:S(2)}) collective-permute-start(bf16[2,128,128]{2,1,0:T(8,128)(2,1)} %get-tuple-element.1740), channel_id=1, source_target_pairs={{0,8},{8,16},{16,24},{24,32},{32,40},{40,48},{48,56},{56,64},{64,7... | collective-permute-start | bytes 196616 | tf_op jit(solution)/shard_map/while/body/eval_jaxpr/ppermute | solution.py:59
  107.0 5.8 %collective-permute-start = (bf16[2,128,128]{2,1,0:T(8,128)(2,1)}, bf16[2,128,128]{2,1,0:T(8,128)(2,1)S(1)}, u32[]{:S(2)}, u32[]{:S(2)}) collective-permute-start(bf16[2,128,128]{2,1,0:T(8,128)(2,1)} %get-tuple-element.1740), channel_id=1, source_target_pairs={{0,8},{8,16},{16,24},{24,32},{32,40},{40,48},{48,56},{56,64},{64,7... | collective-permute-start | bytes 196616 | tf_op jit(solution)/shard_map/while/body/eval_jaxpr/ppermute | solution.py:59
  119.9 5.8 %collective-permute-start = (bf16[2,128,128]{2,1,0:T(8,128)(2,1)}, bf16[2,128,128]{2,1,0:T(8,128)(2,1)S(1)}, u32[]{:S(2)}, u32[]{:S(2)}) collective-permute-start(bf16[2,128,128]{2,1,0:T(8,128)(2,1)} %get-tuple-element.1740), channel_id=1, source_target_pairs={{0,8},{8,16},{16,24},{24,32},{32,40},{40,48},{48,56},{56,64},{64,7... | collective-permute-start | bytes 196616 | tf_op jit(solution)/shard_map/while/body/eval_jaxpr/ppermute | solution.py:59
  126.4 7.0 %collective-permute-start = (bf16[2,128,128]{2,1,0:T(8,128)(2,1)}, bf16[2,128,128]{2,1,0:T(8,128)(2,1)S(1)}, u32[]{:S(2)}, u32[]{:S(2)}) collective-permute-start(bf16[2,128,128]{2,1,0:T(8,128)(2,1)} %get-tuple-element.1740), channel_id=1, source_target_pairs={{0,8},{8,16},{16,24},{24,32},{32,40},{40,48},{48,56},{56,64},{64,7... | collective-permute-start | bytes 196616 | tf_op jit(solution)/shard_map/while/body/eval_jaxpr/ppermute | solution.py:59
  134.1 7.0 %collective-permute-start = (bf16[2,128,128]{2,1,0:T(8,128)(2,1)}, bf16[2,128,128]{2,1,0:T(8,128)(2,1)S(1)}, u32[]{:S(2)}, u32[]{:S(2)}) collective-permute-start(bf16[2,128,128]{2,1,0:T(8,128)(2,1)} %get-tuple-element.1740), channel_id=1, source_target_pairs={{0,8},{8,16},{16,24},{24,32},{32,40},{40,48},{48,56},{56,64},{64,7... | collective-permute-start | bytes 196616 | tf_op jit(solution)/shard_map/while/body/eval_jaxpr/ppermute | solution.py:59
  141.7 7.0 %collective-permute-start = (bf16[2,128,128]{2,1,0:T(8,128)(2,1)}, bf16[2,128,128]{2,1,0:T(8,128)(2,1)S(1)}, u32[]{:S(2)}, u32[]{:S(2)}) collective-permute-start(bf16[2,128,128]{2,1,0:T(8,128)(2,1)} %get-tuple-element.1740), channel_id=1, source_target_pairs={{0,8},{8,16},{16,24},{24,32},{32,40},{40,48},{48,56},{56,64},{64,7... | collective-permute-start | bytes 196616 | tf_op jit(solution)/shard_map/while/body/eval_jaxpr/ppermute | solution.py:59
  149.4 7.0 %collective-permute-start = (bf16[2,128,128]{2,1,0:T(8,128)(2,1)}, bf16[2,128,128]{2,1,0:T(8,128)(2,1)S(1)}, u32[]{:S(2)}, u32[]{:S(2)}) collective-permute-start(bf16[2,128,128]{2,1,0:T(8,128)(2,1)} %get-tuple-element.1740), channel_id=1, source_target_pairs={{0,8},{8,16},{16,24},{24,32},{32,40},{40,48},{48,56},{56,64},{64,7... | collective-permute-start | bytes 196616 | tf_op jit(solution)/shard_map/while/body/eval_jaxpr/ppermute | solution.py:59
  157.1 7.0 %collective-permute-start = (bf16[2,128,128]{2,1,0:T(8,128)(2,1)}, bf16[2,128,128]{2,1,0:T(8,128)(2,1)S(1)}, u32[]{:S(2)}, u32[]{:S(2)}) collective-permute-start(bf16[2,128,128]{2,1,0:T(8,128)(2,1)} %get-tuple-element.1740), channel_id=1, source_target_pairs={{0,8},{8,16},{16,24},{24,32},{32,40},{40,48},{48,56},{56,64},{64,7... | collective-permute-start | bytes 196616 | tf_op jit(solution)/shard_map/while/body/eval_jaxpr/ppermute | solution.py:59
  164.7 7.0 %collective-permute-start = (bf16[2,128,128]{2,1,0:T(8,128)(2,1)}, bf16[2,128,128]{2,1,0:T(8,128)(2,1)S(1)}, u32[]{:S(2)}, u32[]{:S(2)}) collective-permute-start(bf16[2,128,128]{2,1,0:T(8,128)(2,1)} %get-tuple-element.1740), channel_id=1, source_target_pairs={{0,8},{8,16},{16,24},{24,32},{32,40},{40,48},{48,56},{56,64},{64,7... | collective-permute-start | bytes 196616 | tf_op jit(solution)/shard_map/while/body/eval_jaxpr/ppermute | solution.py:59
  172.4 7.0 %collective-permute-start = (bf16[2,128,128]{2,1,0:T(8,128)(2,1)}, bf16[2,128,128]{2,1,0:T(8,128)(2,1)S(1)}, u32[]{:S(2)}, u32[]{:S(2)}) collective-permute-start(bf16[2,128,128]{2,1,0:T(8,128)(2,1)} %get-tuple-element.1740), channel_id=1, source_target_pairs={{0,8},{8,16},{16,24},{24,32},{32,40},{40,48},{48,56},{56,64},{64,7... | collective-permute-start | bytes 196616 | tf_op jit(solution)/shard_map/while/body/eval_jaxpr/ppermute | solution.py:59
  180.1 7.0 %collective-permute-start = (bf16[2,128,128]{2,1,0:T(8,128)(2,1)}, bf16[2,128,128]{2,1,0:T(8,128)(2,1)S(1)}, u32[]{:S(2)}, u32[]{:S(2)}) collective-permute-start(bf16[2,128,128]{2,1,0:T(8,128)(2,1)} %get-tuple-element.1740), channel_id=1, source_target_pairs={{0,8},{8,16},{16,24},{24,32},{32,40},{40,48},{48,56},{56,64},{64,7... | collective-permute-start | bytes 196616 | tf_op jit(solution)/shard_map/while/body/eval_jaxpr/ppermute | solution.py:59
  187.7 7.0 %collective-permute-start = (bf16[2,128,128]{2,1,0:T(8,128)(2,1)}, bf16[2,128,128]{2,1,0:T(8,128)(2,1)S(1)}, u32[]{:S(2)}, u32[]{:S(2)}) collective-permute-start(bf16[2,128,128]{2,1,0:T(8,128)(2,1)} %get-tuple-element.1740), channel_id=1, source_target_pairs={{0,8},{8,16},{16,24},{24,32},{32,40},{40,48},{48,56},{56,64},{64,7... | collective-permute-start | bytes 196616 | tf_op jit(solution)/shard_map/while/body/eval_jaxpr/ppermute | solution.py:59
  195.4 7.0 %collective-permute-start = (bf16[2,128,128]{2,1,0:T(8,128)(2,1)}, bf16[2,128,128]{2,1,0:T(8,128)(2,1)S(1)}, u32[]{:S(2)}, u32[]{:S(2)}) collective-permute-start(bf16[2,128,128]{2,1,0:T(8,128)(2,1)} %get-tuple-element.1740), channel_id=1, source_target_pairs={{0,8},{8,16},{16,24},{24,32},{32,40},{40,48},{48,56},{56,64},{64,7... | collective-permute-start | bytes 196616 | tf_op jit(solution)/shard_map/while/body/eval_jaxpr/ppermute | solution.py:59
  203.1 7.0 %collective-permute-start = (bf16[2,128,128]{2,1,0:T(8,128)(2,1)}, bf16[2,128,128]{2,1,0:T(8,128)(2,1)S(1)}, u32[]{:S(2)}, u32[]{:S(2)}) collective-permute-start(bf16[2,128,128]{2,1,0:T(8,128)(2,1)} %get-tuple-element.1740), channel_id=1, source_target_pairs={{0,8},{8,16},{16,24},{24,32},{32,40},{40,48},{48,56},{56,64},{64,7... | collective-permute-start | bytes 196616 | tf_op jit(solution)/shard_map/while/body/eval_jaxpr/ppermute | solution.py:59
  210.7 7.0 %collective-permute-start = (bf16[2,128,128]{2,1,0:T(8,128)(2,1)}, bf16[2,128,128]{2,1,0:T(8,128)(2,1)S(1)}, u32[]{:S(2)}, u32[]{:S(2)}) collective-permute-start(bf16[2,128,128]{2,1,0:T(8,128)(2,1)} %get-tuple-element.1740), channel_id=1, source_target_pairs={{0,8},{8,16},{16,24},{24,32},{32,40},{40,48},{48,56},{56,64},{64,7... | collective-permute-start | bytes 196616 | tf_op jit(solution)/shard_map/while/body/eval_jaxpr/ppermute | solution.py:59
  218.4 7.0 %collective-permute-start = (bf16[2,128,128]{2,1,0:T(8,128)(2,1)}, bf16[2,128,128]{2,1,0:T(8,128)(2,1)S(1)}, u32[]{:S(2)}, u32[]{:S(2)}) collective-permute-start(bf16[2,128,128]{2,1,0:T(8,128)(2,1)} %get-tuple-element.1740), channel_id=1, source_target_pairs={{0,8},{8,16},{16,24},{24,32},{32,40},{40,48},{48,56},{56,64},{64,7... | collective-permute-start | bytes 196616 | tf_op jit(solution)/shard_map/while/body/eval_jaxpr/ppermute | solution.py:59
  226.0 7.0 %collective-permute-start = (bf16[2,128,128]{2,1,0:T(8,128)(2,1)}, bf16[2,128,128]{2,1,0:T(8,128)(2,1)S(1)}, u32[]{:S(2)}, u32[]{:S(2)}) collective-permute-start(bf16[2,128,128]{2,1,0:T(8,128)(2,1)} %get-tuple-element.1740), channel_id=1, source_target_pairs={{0,8},{8,16},{16,24},{24,32},{32,40},{40,48},{48,56},{56,64},{64,7... | collective-permute-start | bytes 196616 | tf_op jit(solution)/shard_map/while/body/eval_jaxpr/ppermute | solution.py:59
  233.7 7.0 %collective-permute-start = (bf16[2,128,128]{2,1,0:T(8,128)(2,1)}, bf16[2,128,128]{2,1,0:T(8,128)(2,1)S(1)}, u32[]{:S(2)}, u32[]{:S(2)}) collective-permute-start(bf16[2,128,128]{2,1,0:T(8,128)(2,1)} %get-tuple-element.1740), channel_id=1, source_target_pairs={{0,8},{8,16},{16,24},{24,32},{32,40},{40,48},{48,56},{56,64},{64,7... | collective-permute-start | bytes 196616 | tf_op jit(solution)/shard_map/while/body/eval_jaxpr/ppermute | solution.py:59
  241.4 7.0 %collective-permute-start = (bf16[2,128,128]{2,1,0:T(8,128)(2,1)}, bf16[2,128,128]{2,1,0:T(8,128)(2,1)S(1)}, u32[]{:S(2)}, u32[]{:S(2)}) collective-permute-start(bf16[2,128,128]{2,1,0:T(8,128)(2,1)} %get-tuple-element.1740), channel_id=1, source_target_pairs={{0,8},{8,16},{16,24},{24,32},{32,40},{40,48},{48,56},{56,64},{64,7... | collective-permute-start | bytes 196616 | tf_op jit(solution)/shard_map/while/body/eval_jaxpr/ppermute | solution.py:59
  413.8 20.2 %all-to-all-start.6 = ((f32[16,8,1024]{2,1,0:T(8,128)}), f32[16,8,1024]{2,1,0:T(8,128)S(1)}, u32[]{:S(2)}, u32[]{:S(2)}) async-start(f32[16,8,1024]{2,1,0:T(8,128)} %reduce_sum.128), calls=%async_computation.6 | async-start | bytes 1048576 | tf_op jit(solution)/shard_map/all_to_all | solution.py:70
  434.9 89.9 %all-to-all-start.7 = ((f32[16,8,1024]{2,1,0:T(8,128)}), f32[16,8,1024]{2,1,0:T(8,128)S(1)}, u32[]{:S(2)}, u32[]{:S(2)}) async-start(f32[16,8,1024]{2,1,0:T(8,128)} %broadcast_in_dim.62), calls=%async_computation.7 | async-start | bytes 1048576 | tf_op jit(solution)/shard_map/all_to_all | solution.py:24
  (18 other events, 153.4 us)
where the time goes:
time: 540 us; the launch traced here: 530 us
  waiting for transfers between devices  174 us (32%)
  matrix products  147 us (27%)
  blocking collectives  83.5 us (15%)
  starting transfers between devices  70.6 us (13%)
  local copies, waits for them, and re-layouts  34.5 us (6%)
  other arithmetic  10.8 us (2%)
  loops' own time  8.84 us (2%)
    ppermute x31, waiting for transfers between devices, shifted(): lax.ppermute(value, axis, [(source, source + steps) for source in range(f...  156 us
    dot_general x64, matrix products, block_scores(): jnp.einsum('grd,ngd->grn', grad_rows, value_block, preferred_element_type...  62.3 us
    all_to_all x3, blocking collectives, from_everyone(): return lax.all_to_all(copies, axis, split_axis=0, concat_axis=0, tiled=True)  52 us
    dot_general x32, matrix products, backward_update(): jnp.einsum('grn,ngd->grd', score_grad, key_block, preferred_element_type=...  44 us
    ppermute x31, starting transfers between devices, shifted(): lax.ppermute(value, axis, [(source, source + steps) for source in range(f...  40.1 us
    dot_general x32, matrix products, block_scores(): jnp.einsum('grd,ngd->grn', query_rows, key_block, preferred_element_type=...  32.1 us
    all_to_all x2, blocking collectives, sum_at_owner(): parts = lax.all_to_all(in_blocks(value, dim, count), axis, 0, 0, tiled=True)  31.4 us
    while x31, local copies, waits for them, and re-layouts  19.5 us
  transfers between devices with their start and end apart: 35, of which 33 were waited for; matrix products, arithmetic and copies ran while one was open for 20% of the time, Pallas kernels for 0%

commit v1 on v0

v1 whole, which is shorter than its diff:
```python
import math

import jax
import jax.numpy as jnp
from jax import lax
from jax.experimental import pallas as pl
from jax.experimental.pallas import tpu as pltpu
from jax.sharding import Mesh
from jax.sharding import PartitionSpec as P

HD = 128
SCALE = 1.0 / math.sqrt(HD)
LOG2E = math.log2(math.e)
C1 = SCALE * LOG2E
NEG = -1e30
SEQ = ("y", "z", "c")
YZ = ("y", "z")
CYZ = ("c", "y", "z")
HEAD = ("x", "w")
OWNERS = ("x", "w", "y", "z")
F32 = jnp.float32
BF16 = jnp.bfloat16


def dot_nt(a, b):
    return lax.dot_general(a, b, (((1,), (1,)), ((), ())), preferred_element_type=F32)


def dot_nn(a, b):
    return lax.dot_general(a, b, (((1,), (0,)), ((), ())), preferred_element_type=F32)


def dot_tn(a, b):
    return lax.dot_general(a, b, (((0,), (0,)), ((), ())), preferred_element_type=F32)


def stats_kernel(pos, q, g, own_k, own_v, mine, other, pkv, grads, stats, q2, g2):
    rows = own_k.shape[0]
    heads = q.shape[1] // HD
    tile = 2 * HD
    tiles = heads * rows // tile
    npre = pkv.shape[1]
    here = pos[0]
    core = pos[1]
    for h in range(heads):
        q2[h * rows : (h + 1) * rows, :] = q[:, h * HD : (h + 1) * HD]
        g2[h * rows : (h + 1) * rows, :] = g[:, h * HD : (h + 1) * HD]

    def update(state, s, d):
        m, l, t = state
        n = s.shape[0] // 8
        s = s.reshape(n, 8, tile)
        d = d.reshape(n, 8, tile)
        new = jnp.maximum(m, jnp.max(s, axis=0))
        fade = jnp.exp2(m - new)
        w = jnp.exp2(s - new[None])
        return (new, l * fade + jnp.sum(w, axis=0), t * fade + jnp.sum(w * d, axis=0))

    def tile_of(r):
        return slice(r * tile, (r + 1) * tile)

    def sweep(i, states):
        kc = jnp.concatenate([mine[i, 0], other[i, 0]], 0)
        vc = jnp.concatenate([mine[i, 1], other[i, 1]], 0)
        out = []
        for r in range(tiles):
            s = dot_nt(kc, q2[tile_of(r), :]) * C1
            d = dot_nt(vc, g2[tile_of(r), :])
            out.append(update(states[r], s, d))
        return tuple(out)

    zero = jnp.zeros((8, tile), F32)
    states = tuple((jnp.full((8, tile), NEG, F32), zero, zero) for _ in range(tiles))
    states = lax.fori_loop(0, here, sweep, states)
    kc = jnp.concatenate([own_k[...], other[here, 0]], 0)
    vc = jnp.concatenate([own_v[...], other[here, 1]], 0)
    key = lax.broadcasted_iota(jnp.int32, (2 * rows, tile), 0)
    row = lax.broadcasted_iota(jnp.int32, (2 * rows, tile), 1) % rows
    bound = jnp.where(key < rows, row, rows - 1 + core * rows)
    seen = key <= bound
    kg = jnp.zeros((npre, HD), F32)
    vg = jnp.zeros((npre, HD), F32)
    for r in range(tiles):
        s = jnp.where(seen, dot_nt(kc, q2[tile_of(r), :]) * C1, NEG)
        d = dot_nt(vc, g2[tile_of(r), :])
        state = update(states[r], s, d)
        s = dot_nt(pkv[0], q2[tile_of(r), :]) * C1
        d = dot_nt(pkv[1], g2[tile_of(r), :])
        m, l, t = update(state, s, d)
        top = jnp.max(m, axis=0, keepdims=True)
        fade = jnp.exp2(m - top)
        total = jnp.sum(l * fade, axis=0, keepdims=True)
        delta = jnp.sum(t * fade, axis=0, keepdims=True) / total
        log_total = top + jnp.log2(total)
        stats[0:1, tile_of(r)] = log_total
        stats[1:2, tile_of(r)] = delta
        p = jnp.exp2(s - log_total)
        ds = (p * (d - delta)).astype(BF16)
        kg = kg + dot_nn(ds, q2[tile_of(r), :])
        vg = vg + dot_nn(p.astype(BF16), g2[tile_of(r), :])
    grads[0] = (kg * SCALE).astype(grads.dtype)
    grads[1] = vg.astype(grads.dtype)


def grad_kernel(pos, q, g, stats, own_k, own_v, mine, other, pkv, *rest):
    out, q2, g2, lt, de = rest[-5:]
    rows = own_k.shape[0]
    heads = q.shape[1] // HD
    tile = heads * rows
    here = pos[0]
    core = pos[1]
    for h in range(heads):
        span = slice(h * rows, (h + 1) * rows)
        q2[span, :] = q[:, h * HD : (h + 1) * HD]
        g2[span, :] = g[:, h * HD : (h + 1) * HD]
    lt[...] = jnp.broadcast_to(stats[:, 0:1], (tile, HD))
    de[...] = jnp.broadcast_to(stats[:, 1:2], (tile, HD))

    def part(kc, vc, seen=None):
        s = dot_nt(q2[...], kc) * C1
        d = dot_nt(g2[...], vc)
        if seen is not None:
            s = jnp.where(seen, s, NEG)
        pieces = []
        for b in range(kc.shape[0] // HD):
            lanes = slice(b * HD, (b + 1) * HD)
            p = jnp.exp2(s[:, lanes] - lt[...])
            pieces.append((p * (d[:, lanes] - de[...])).astype(BF16))
        return dot_nn(jnp.concatenate(pieces, 1), kc)

    def sweep(i, total):
        kc = jnp.concatenate([mine[i, 0], other[i, 0]], 0)
        vc = jnp.concatenate([mine[i, 1], other[i, 1]], 0)
        return total + part(kc, vc)

    total = part(pkv[0], pkv[1])
    total = lax.fori_loop(0, here, sweep, total)
    kc = jnp.concatenate([own_k[...], other[here, 0]], 0)
    vc = jnp.concatenate([own_v[...], other[here, 1]], 0)
    key = lax.broadcasted_iota(jnp.int32, (tile, 2 * rows), 1)
    row = lax.broadcasted_iota(jnp.int32, (tile, 2 * rows), 0) % rows
    bound = jnp.where(key < rows, row, rows - 1 + core * rows)
    total = (total + part(kc, vc, key <= bound)) * SCALE
    for h in range(heads):
        out[:, h * HD : (h + 1) * HD] = total[h * rows : (h + 1) * rows].astype(out.dtype)


def whole(shape):
    return pl.BlockSpec(shape, lambda *_: (0,) * len(shape))


def attention_stats(pos, q, g, own_k, own_v, mine, other, pkv):
    rows, width = q.shape
    n = rows * width // HD
    return pl.pallas_call(
        stats_kernel,
        out_shape=(
            jax.ShapeDtypeStruct(pkv.shape, BF16),
            jax.ShapeDtypeStruct((2, n), F32),
        ),
        in_specs=[pl.BlockSpec(memory_space=pltpu.SMEM)]
        + [whole(v.shape) for v in (q, g, own_k, own_v, mine, other, pkv)],
        out_specs=(whole(pkv.shape), whole((2, n))),
        grid=(1,),
        scratch_shapes=[
            pltpu.VMEM((n, HD), BF16),
            pltpu.VMEM((n, HD), BF16),
        ],
        cost_estimate=pl.CostEstimate(flops=3 * 10**9, bytes_accessed=3 * 10**6, transcendentals=4 * 10**6),
        name="stats",
    )(pos, q, g, own_k, own_v, mine, other, pkv)


def query_grad_piece(piece, count, pos, q, g, stats, own_k, own_v, mine, other, pkv, *prior):
    rows, width = q.shape
    part = width // count
    tile = part // HD * rows
    block = pl.BlockSpec((rows, part), lambda *_: (0, piece))
    return pl.pallas_call(
        grad_kernel,
        out_shape=jax.ShapeDtypeStruct(q.shape, BF16),
        in_specs=[
            pl.BlockSpec(memory_space=pltpu.SMEM),
            block,
            block,
            pl.BlockSpec((tile, 2), lambda *_: (piece, 0)),
        ]
        + [whole(v.shape) for v in (own_k, own_v, mine, other, pkv)]
        + [pl.BlockSpec(memory_space=pl.ANY) for _ in prior],
        out_specs=block,
        grid=(1,),
        scratch_shapes=[
            pltpu.VMEM((tile, HD), BF16),
            pltpu.VMEM((tile, HD), BF16),
            pltpu.VMEM((tile, HD), F32),
            pltpu.VMEM((tile, HD), F32),
        ],
        input_output_aliases={9: 0} if prior else {},
        cost_estimate=pl.CostEstimate(flops=10**9, bytes_accessed=3 * 10**6, transcendentals=10**6),
        name="query_grad",
    )(pos, q, g, stats, own_k, own_v, mine, other, pkv, *prior)


def exchange(value, axes):
    return lax.all_to_all(value, axes, 0, 0, tiled=True)


def to_all(value, axes):
    return exchange(jnp.broadcast_to(value, (lax.axis_size(axes), *value.shape)), axes)


def sum_parts(value, axes, dtype=BF16):
    count = lax.axis_size(axes)
    parts = exchange(value.reshape(count, -1, HD).astype(dtype), axes)
    return jnp.sum(parts.astype(F32), axis=0)


def sum_everywhere(value):
    own = sum_parts(value, SEQ).astype(BF16)
    return to_all(own, SEQ).reshape(value.shape)


def swap_cores(value):
    return lax.ppermute(value, "c", [(0, 1), (1, 0)])


def on_device(prefix_embed, w_hidden, b_hidden, w_out, queries, keys, values, out_grad):
    npre, emb = prefix_embed.shape
    units = w_hidden.shape[1]
    core = lax.axis_index("c")
    here = lax.axis_index(YZ)
    head = lax.axis_index(HEAD)
    heads = lax.axis_size(HEAD)
    pos = jnp.stack([here, core]).astype(jnp.int32)

    mine = to_all(jnp.stack([keys, values], 0), YZ)
    hidden_pre = jnp.dot(prefix_embed, w_hidden, preferred_element_type=F32) + b_hidden
    tangent = jnp.tanh(hidden_pre)
    hidden = tangent.astype(BF16)
    partial_kv = jnp.einsum("ph,hck->cpk", hidden, w_out, preferred_element_type=F32)
    pkv = sum_everywhere(partial_kv)
    other = swap_cores(mine)
    grads, stats = attention_stats(pos, queries, out_grad, keys, values, mine, other, pkv)
    columns = stats.T
    prefix_grads = sum_everywhere(grads)
    query_grad = ()
    count = 4
    for piece in range(count):
        query_grad = (
            query_grad_piece(
                piece, count, pos, queries, out_grad, columns, keys, values, mine, other, pkv, *query_grad
            ),
        )
    grad_w_out = jnp.einsum("ph,cpk->hck", hidden, prefix_grads, preferred_element_type=F32)
    hidden_part = jnp.einsum("cpk,hck->ph", prefix_grads, w_out, preferred_element_type=F32)
    share = npre // heads
    parts = exchange(hidden_part.reshape(heads, share, units), HEAD)
    hidden_grad = jnp.sum(parts, axis=0)
    own_tangent = lax.dynamic_slice_in_dim(tangent, head * share, share, 0)
    pre_part = (hidden_grad * (1.0 - own_tangent * own_tangent)).astype(BF16)
    embed_part = dot_nt(pre_part, w_hidden)
    own = sum_parts(embed_part, CYZ)
    near = to_all(own.astype(BF16), OWNERS)
    far = swap_cores(near)
    sides = jnp.stack([jnp.where(core == 0, near, far), jnp.where(core == 0, far, near)], 0)
    sides = sides.reshape(2, heads, -1, emb).transpose(1, 0, 2, 3)
    grad_prefix = sides.reshape(npre, emb).astype(F32)
    pre_rounded = to_all(pre_part, HEAD).reshape(npre, units)
    grad_w_hidden = dot_tn(prefix_embed, pre_rounded)
    grad_b_hidden = jnp.sum(pre_rounded.astype(F32), axis=0)
    return (*query_grad, grad_w_out, grad_w_hidden, grad_b_hidden, grad_prefix)


def solution(mesh):
    torus = Mesh(mesh.devices.reshape(2, 8, 2, 4, 2), ("y", "z", "c", "x", "w"))
    placed = (
        P(),
        P(None, SEQ),
        P(SEQ),
        P(SEQ, None, HEAD),
        P(SEQ, HEAD),
        P(SEQ, HEAD),
        P(SEQ, HEAD),
        P(SEQ, HEAD),
    )
    return jax.shard_map(
        on_device,
        mesh=torus,
        in_specs=placed,
        out_specs=(P(SEQ, HEAD), P(SEQ, None, HEAD), P(None, SEQ), P(SEQ), P()),
        check_vma=False,
    )
```

time: 540 us -> 196 us (0.36); the launches traced: 530 us -> 193 us
  waiting for transfers between devices: 174 us -> 18.3 us
  matrix products: 147 us -> 2.2 us
  Pallas kernels: 0 us -> 47.9 us
  starting transfers between devices: 70.6 us -> 32.2 us
  local copies, waits for them, and re-layouts: 34.5 us -> 6.88 us
  loops' own time: 8.84 us -> 0 us
  other arithmetic: 10.8 us -> 3.24 us
    ppermute x31 -> x2, waiting for transfers between devices: 156 us -> 0.01 us  [swap_cores(): return lax.ppermute(value, 'c', [(0, 1), (1, 0)])]
    dot_general x139 -> x6, matrix products: 147 us -> 2.2 us  [the longest x1 0.93 us: on_device(): jnp.einsum('cpk,hck->ph', prefix_grads, w_out, preferred_element_type=F32)]
    pallas_call x0 -> x5, Pallas kernels: none -> 47.9 us  [the longest x4 35.6 us: query_grad_piece(): pl.pallas_call(grad_kernel, out_shape=jax.ShapeDtypeStruct(q.shape, BF16)...]
    ppermute x31 -> x2, starting transfers between devices: 40.1 us -> 3.78 us  [swap_cores(): return lax.ppermute(value, 'c', [(0, 1), (1, 0)])]
    while x31 -> x0, local copies, waits for them, and re-layouts: 19.5 us -> none
    another operation x67 -> x0, loops' own time: 8.84 us -> none  [the longest x64 4.14 us: advance(): lax.cond(useful, lambda kept: update(kept, key_block, value_block, first_...]
    reduce_sum x38 -> x5, other arithmetic: 7.36 us -> 0.74 us  [the longest x1 0.61 us: on_device(): grad_b_hidden = jnp.sum(pre_rounded.astype(F32), axis=0)]
  transfers between devices with their start and end apart: 35 -> 6, of which waited for: 33 -> 3; matrix products, arithmetic and copies ran while one was open for 20% -> 3% of each run, Pallas kernels for 0% -> 18%
where the time goes in v1:
time: 196 us; the launch traced here: 193 us
  blocking collectives  81.8 us (42%)
  Pallas kernels  47.9 us (24%)
  starting transfers between devices  32.2 us (16%)
  waiting for transfers between devices  18.3 us (9%)
  local copies, waits for them, and re-layouts  6.88 us (4%)
  other arithmetic  3.24 us (2%)
  matrix products  2.2 us (1%)
    all_to_all x5, blocking collectives, exchange(): return lax.all_to_all(value, axes, 0, 0, tiled=True)  81.8 us
    pallas_call x4, Pallas kernels, query_grad_piece(): pl.pallas_call(grad_kernel, out_shape=jax.ShapeDtypeStruct(q.shape, BF16)...  35.6 us
    all_to_all x4, starting transfers between devices, exchange(): return lax.all_to_all(value, axes, 0, 0, tiled=True)  28.4 us
    all_to_all x4, waiting for transfers between devices, exchange(): return lax.all_to_all(value, axes, 0, 0, tiled=True)  18.3 us
    pallas_call x1, Pallas kernels, attention_stats(): pl.pallas_call(stats_kernel, out_shape=(jax.ShapeDtypeStruct(pkv.shape, B...  12.2 us
  transfers between devices with their start and end apart: 6, of which 3 were waited for; matrix products, arithmetic and copies ran while one was open for 3% of the time, Pallas kernels for 18%

profile of v1, /device:TPU:233, one launch (start us, length us, event | category | flops | bytes accessed | tf_op | source)
XLA Modules:
  0.0 193.3 jit_solution(3406849037254545978)
XLA Ops:
  0.6 0.8 pad_maximum_fusion
  1.7 30.7 %all_to_all.45.mine = bf16[16,2,128,128]{3,2,1,0:T(8,128)(2,1)S(1)} all-to-all(bf16[16,2,128,128]{3,2,1,0:T(8,128)(2,1)S(1)} %broadcast_in_dim.16), channel_id=1, replica_groups=mesh['y'=2,'z'=8,'c'=2,'x'=4,'w'=2] {'y','z'}, dimensions={0} | all-to-all | bytes 2097152 | tf_op jit(solution)/shard_map/all_to_all | solution.py:205
  32.4 2.4 %collective-permute-start = (bf16[16,2,128,128]{3,2,1,0:T(8,128)(2,1)S(1)}, bf16[16,2,128,128]{3,2,1,0:T(8,128)(2,1)S(1)}, u32[]{:S(2)}, u32[]{:S(2)}) collective-permute-start(bf16[16,2,128,128]{3,2,1,0:T(8,128)(2,1)S(1)} %all_to_all.45.mine), channel_id=1, source_target_pairs={{0,8},{8,0},{1,9},{9,1},{2,10},{10,2},{3,11},{11,3},{4,12},{12,4},... | collective-permute-start | bytes 3145736 | tf_op jit(solution)/shard_map/ppermute | solution.py:224
  35.3 12.5 %all_to_all.46 = bf16[32,16,128]{2,1,0:T(8,128)(2,1)S(1)} all-to-all(bf16[32,16,128]{2,1,0:T(8,128)(2,1)S(1)} %bitcast.56), channel_id=1, replica_groups=mesh['y'=2,'z'=8,'c'=2,'x'=4,'w'=2] {'y','z','c'}, dimensions={0} | all-to-all | bytes 262144 | tf_op jit(solution)/shard_map/all_to_all | solution.py:205
  47.9 0.7 broadcast_in_dim.17
  48.6 7.9 %all-to-all-start.2 = ((bf16[32,16,128]{2,1,0:T(8,128)(2,1)}), bf16[32,16,128]{2,1,0:T(8,128)(2,1)S(1)}, u32[]{:S(2)}, u32[]{:S(2)}) async-start(bf16[32,16,128]{2,1,0:T(8,128)(2,1)} %broadcast_in_dim.17), calls=%async_computation.2 | async-start | bytes 262144 | tf_op jit(solution)/shard_map/all_to_all | solution.py:205
  56.5 0.6 pad_add_fusion.pos
  57.0 5.8 %all-to-all-done.2 = bf16[32,16,128]{2,1,0:T(8,128)(2,1)S(1)} async-done(((bf16[32,16,128]{2,1,0:T(8,128)(2,1)}), bf16[32,16,128]{2,1,0:T(8,128)(2,1)S(1)}, u32[]{:S(2)}, u32[]{:S(2)}) %all-to-all-start.2) | async-done | bytes 131104 | tf_op jit(solution)/shard_map/all_to_all | solution.py:205
  62.8 0.6 copy-done.3
  63.4 0.4 copy-done.2
  63.8 12.2 %stats.1 = (bf16[2,256,128]{2,1,0:T(8,128)(2,1)}, f32[2,1024]{1,0:T(2,128)}) custom-call(s32[2]{0:T(128)} %pad_add_fusion.pos, bf16[128,1024]{1,0:T(8,128)(2,1)} %q.9, bf16[128,1024]{1,0:T(8,128)(2,1)} %g.9, bf16[128,128]{1,0:T(8,128)(2,1)} %own_k.9, bf16[128,128]{1,0:T(8,128)(2,1)} %own_v.9, bf16[16,2,128,128]{3,2,1,0:T(8,128)(2,1)} %copy-done.1, ...), custom_call_target="tpu_custom_call" | custom-call | flops 3000000000 | bytes 3000000 | tf_op jit(solution)/shard_map/stats/pallas_call | solution.py:155
  76.1 12.2 %all_to_all.47 = bf16[32,16,128]{2,1,0:T(8,128)(2,1)S(1)} all-to-all(bf16[32,16,128]{2,1,0:T(8,128)(2,1)} %bitcast.59), channel_id=1, replica_groups=mesh['y'=2,'z'=8,'c'=2,'x'=4,'w'=2] {'y','z','c'}, dimensions={0} | all-to-all | bytes 262144 | tf_op jit(solution)/shard_map/all_to_all | solution.py:205
  88.3 13.4 %all_to_all.48 = bf16[32,16,128]{2,1,0:T(8,128)(2,1)S(1)} all-to-all(bf16[32,16,128]{2,1,0:T(8,128)(2,1)S(1)} %broadcast_in_dim.18), channel_id=1, replica_groups=mesh['y'=2,'z'=8,'c'=2,'x'=4,'w'=2] {'y','z','c'}, dimensions={0} | all-to-all | bytes 262144 | tf_op jit(solution)/shard_map/all_to_all | solution.py:205
  101.7 0.9 convolution_bitcast_fusion.1
  102.7 5.8 %all-to-all-start.5 = ((f32[8,32,256]{2,1,0:T(8,128)}), f32[8,32,256]{2,1,0:T(8,128)S(1)}, u32[]{:S(2)}, u32[]{:S(2)}) async-start(f32[8,32,256]{2,1,0:T(8,128)} %convolution_bitcast_fusion.1), calls=%async_computation.5 | async-start | bytes 524288 | tf_op jit(solution)/shard_map/all_to_all | solution.py:205
  108.4 8.2 %all-to-all-done.5 = f32[8,32,256]{2,1,0:T(8,128)S(1)} async-done(((f32[8,32,256]{2,1,0:T(8,128)}), f32[8,32,256]{2,1,0:T(8,128)S(1)}, u32[]{:S(2)}, u32[]{:S(2)}) %all-to-all-start.5) | async-done | bytes 262176 | tf_op jit(solution)/shard_map/all_to_all | solution.py:205
  117.0 13.0 %all_to_all.49 = bf16[32,8,128]{2,1,0:T(8,128)(2,1)S(1)} all-to-all(bf16[32,8,128]{2,1,0:T(8,128)(2,1)S(1)} %bitcast.58), channel_id=1, replica_groups=mesh['y'=2,'z'=8,'c'=2,'x'=4,'w'=2] {'c','y','z'}, dimensions={0} | all-to-all | bytes 131072 | tf_op jit(solution)/shard_map/all_to_all | solution.py:205
  130.1 0.7 broadcast_in_dim.20
  130.8 8.8 %all-to-all-start.8 = ((bf16[128,8,128]{2,1,0:T(8,128)(2,1)}), bf16[128,8,128]{2,1,0:T(8,128)(2,1)S(1)}, u32[]{:S(2)}, u32[]{:S(2)}) async-start(bf16[128,8,128]{2,1,0:T(8,128)(2,1)} %broadcast_in_dim.20), calls=%async_computation.8 | async-start | bytes 524288 | tf_op jit(solution)/shard_map/all_to_all | solution.py:205
  139.6 1.0 copy.24
  140.6 8.9 %query_grad.4.rest_0_ = bf16[128,1024]{1,0:T(8,128)(2,1)} custom-call(s32[2]{0:T(128)} %pad_add_fusion.pos, bf16[128,1024]{1,0:T(8,128)(2,1)} %q.9, bf16[128,1024]{1,0:T(8,128)(2,1)} %g.9, f32[1024,2]{1,0:T(8,128)} %bitcast.41, bf16[128,128]{1,0:T(8,128)(2,1)} %own_k.9, bf16[128,128]{1,0:T(8,128)(2,1)} %own_v.9, bf16[16,2,128,128]{3,2,1,0:T(8,128)(2,1)} %copy-done.1, ...), custom_call_target="tpu_custom_call" | custom-call | flops 1000000000 | bytes 3000000 | tf_op jit(solution)/shard_map/query_grad/pallas_call | solution.py:179
  149.5 8.9 %query_grad.5.rest_0_ = bf16[128,1024]{1,0:T(8,128)(2,1)} custom-call(s32[2]{0:T(128)} %pad_add_fusion.pos, bf16[128,1024]{1,0:T(8,128)(2,1)} %q.9, bf16[128,1024]{1,0:T(8,128)(2,1)} %g.9, f32[1024,2]{1,0:T(8,128)} %bitcast.42, bf16[128,128]{1,0:T(8,128)(2,1)} %own_k.9, bf16[128,128]{1,0:T(8,128)(2,1)} %own_v.9, ...), custom_call_target="tpu_custom_call", output_to_operand_aliasing={{}: (9, {})} | custom-call | flops 1000000000 | bytes 3000000 | tf_op jit(solution)/shard_map/query_grad/pallas_call | solution.py:179
  158.4 8.9 %query_grad.6.rest_0_ = bf16[128,1024]{1,0:T(8,128)(2,1)} custom-call(s32[2]{0:T(128)} %pad_add_fusion.pos, bf16[128,1024]{1,0:T(8,128)(2,1)} %q.9, bf16[128,1024]{1,0:T(8,128)(2,1)} %g.9, f32[1024,2]{1,0:T(8,128)} %bitcast.43, bf16[128,128]{1,0:T(8,128)(2,1)} %own_k.9, bf16[128,128]{1,0:T(8,128)(2,1)} %own_v.9, ...), custom_call_target="tpu_custom_call", output_to_operand_aliasing={{}: (9, {})} | custom-call | flops 1000000000 | bytes 3000000 | tf_op jit(solution)/shard_map/query_grad/pallas_call | solution.py:179
  167.3 8.9 %query_grad.7 = bf16[128,1024]{1,0:T(8,128)(2,1)} custom-call(s32[2]{0:T(128)} %pad_add_fusion.pos, bf16[128,1024]{1,0:T(8,128)(2,1)} %q.9, bf16[128,1024]{1,0:T(8,128)(2,1)} %g.9, f32[1024,2]{1,0:T(8,128)} %bitcast.44, bf16[128,128]{1,0:T(8,128)(2,1)} %own_k.9, bf16[128,128]{1,0:T(8,128)(2,1)} %own_v.9, ...), custom_call_target="tpu_custom_call", output_to_operand_aliasing={{}: (9, {})} | custom-call | flops 1000000000 | bytes 3000000 | tf_op jit(solution)/shard_map/query_grad/pallas_call | solution.py:179
  176.2 0.7 broadcast_in_dim.19
  176.9 6.0 %all-to-all-start.6 = ((bf16[8,32,256]{2,1,0:T(8,128)(2,1)}), bf16[8,32,256]{2,1,0:T(8,128)(2,1)S(1)}, u32[]{:S(2)}, u32[]{:S(2)}) async-start(bf16[8,32,256]{2,1,0:T(8,128)(2,1)} %broadcast_in_dim.19), calls=%async_computation.6 | async-start | bytes 262144 | tf_op jit(solution)/shard_map/all_to_all | solution.py:205
  183.2 0.9 copy.28
  184.1 1.4 collective-permute-start.1
  185.4 4.2 %all-to-all-done.6 = bf16[8,32,256]{2,1,0:T(8,128)(2,1)S(1)} async-done(((bf16[8,32,256]{2,1,0:T(8,128)(2,1)}), bf16[8,32,256]{2,1,0:T(8,128)(2,1)S(1)}, u32[]{:S(2)}, u32[]{:S(2)}) %all-to-all-start.6) | async-done | bytes 131104 | tf_op jit(solution)/shard_map/all_to_all | solution.py:205
  190.0 1.3 copy.29
  191.3 0.6 convert_reduce_fusion
  192.2 1.0 maximum_convert_fusion
  (35 shorter events, 2.0 us)
Async XLA Ops:
  0.6 34.2 %copy-start = (bf16[256,1024]{1,0:T(8,128)(2,1)S(1)}, bf16[256,1024]{1,0:T(8,128)(2,1)}, u32[]{:S(2)}) copy-start(bf16[256,1024]{1,0:T(8,128)(2,1)} %param.8) | copy-start | bytes 1572868
  1.7 33.1 %copy-start.4 = (bf16[1024,256]{1,0:T(8,128)(2,1)S(1)}, bf16[1024,256]{1,0:T(8,128)(2,1)}, u32[]{:S(2)}) copy-start(bf16[1024,256]{1,0:T(8,128)(2,1)} %param.9) | copy-start | bytes 1572868
  1.7 33.1 %copy-start.8 = (f32[256]{0:T(256)S(1)}, f32[256]{0:T(256)}, u32[]{:S(2)}) copy-start(f32[256]{0:T(256)} %param.10) | copy-start | bytes 3076
  32.4 15.5 %copy-start.1 = (bf16[16,2,128,128]{3,2,1,0:T(8,128)(2,1)}, bf16[16,2,128,128]{3,2,1,0:T(8,128)(2,1)S(1)}, u32[]{:S(2)}) copy-start(bf16[16,2,128,128]{3,2,1,0:T(8,128)(2,1)S(1)} %all_to_all.45.mine) | copy-start | bytes 3145732
  32.4 2.7 %copy-start.5 = (bf16[256,2,128]{2,1,0:T(2,128)(2,1)S(1)}, bf16[256,2,128]{2,1,0:T(2,128)(2,1)}, u32[]{:S(2)}) copy-start(bf16[256,2,128]{2,1,0:T(2,128)(2,1)} %param.11) | copy-start | bytes 393220
  32.4 30.4 %collective-permute-start = (bf16[16,2,128,128]{3,2,1,0:T(8,128)(2,1)S(1)}, bf16[16,2,128,128]{3,2,1,0:T(8,128)(2,1)S(1)}, u32[]{:S(2)}, u32[]{:S(2)}) collective-permute-start(bf16[16,2,128,128]{3,2,1,0:T(8,128)(2,1)S(1)} %all_to_all.45.mine), channel_id=1, source_target_pairs={{0,8},{8,0},{1,9},{9,1},{2,10},{10,2},{3,11},{11,3},{4,12},{12,4},... | collective-permute-start | bytes 3145736 | tf_op jit(solution)/shard_map/ppermute | solution.py:224
  48.6 14.2 %all-to-all-start.2 = ((bf16[32,16,128]{2,1,0:T(8,128)(2,1)}), bf16[32,16,128]{2,1,0:T(8,128)(2,1)S(1)}, u32[]{:S(2)}, u32[]{:S(2)}) async-start(bf16[32,16,128]{2,1,0:T(8,128)(2,1)} %broadcast_in_dim.17), calls=%async_computation.2 | async-start | bytes 262144 | tf_op jit(solution)/shard_map/all_to_all | solution.py:205
  62.8 0.6 copy-start.3
  62.8 1.0 copy-start.2
  88.3 13.4 %copy-start.6 = (bf16[256,2,128]{2,1,0:T(2,128)(2,1)S(1)}, bf16[256,2,128]{2,1,0:T(2,128)(2,1)}, u32[]{:S(2)}) copy-start(bf16[256,2,128]{2,1,0:T(2,128)(2,1)} %param.11) | copy-start | bytes 393220
  102.7 14.0 %all-to-all-start.5 = ((f32[8,32,256]{2,1,0:T(8,128)}), f32[8,32,256]{2,1,0:T(8,128)S(1)}, u32[]{:S(2)}, u32[]{:S(2)}) async-start(f32[8,32,256]{2,1,0:T(8,128)} %convolution_bitcast_fusion.1), calls=%async_computation.5 | async-start | bytes 524288 | tf_op jit(solution)/shard_map/all_to_all | solution.py:205
  130.8 8.8 %copy-start.7 = (f32[2,1024]{1,0:T(2,128)S(1)}, f32[2,1024]{1,0:T(2,128)}, u32[]{:S(2)}) copy-start(f32[2,1024]{1,0:T(2,128)} %get-tuple-element.7) | copy-start | bytes 24580
  130.8 45.4 %all-to-all-start.8 = ((bf16[128,8,128]{2,1,0:T(8,128)(2,1)}), bf16[128,8,128]{2,1,0:T(8,128)(2,1)S(1)}, u32[]{:S(2)}, u32[]{:S(2)}) async-start(bf16[128,8,128]{2,1,0:T(8,128)(2,1)} %broadcast_in_dim.20), calls=%async_computation.8 | async-start | bytes 524288 | tf_op jit(solution)/shard_map/all_to_all | solution.py:205
  176.9 12.8 %all-to-all-start.6 = ((bf16[8,32,256]{2,1,0:T(8,128)(2,1)}), bf16[8,32,256]{2,1,0:T(8,128)(2,1)S(1)}, u32[]{:S(2)}, u32[]{:S(2)}) async-start(bf16[8,32,256]{2,1,0:T(8,128)(2,1)} %broadcast_in_dim.19), calls=%async_computation.6 | async-start | bytes 262144 | tf_op jit(solution)/shard_map/all_to_all | solution.py:205
  184.1 7.9 %collective-permute-start.1 = (bf16[128,8,128]{2,1,0:T(8,128)(2,1)S(1)}, bf16[128,8,128]{2,1,0:T(8,128)(2,1)S(1)}, u32[]{:S(2)}, u32[]{:S(2)}) collective-permute-start(bf16[128,8,128]{2,1,0:T(8,128)(2,1)S(1)} %all-to-all-done.8), channel_id=1, source_target_pairs={{0,8},{8,0},{1,9},{9,1},{2,10},{10,2},{3,11},{11,3},{4,12},{12,4},... | collective-permute-start | bytes 786440 | tf_op jit(solution)/shard_map/ppermute | solution.py:224

commit v2 on v1

v2 whole, which is shorter than its diff:
```python
import functools
import math

import jax
import jax.numpy as jnp
from jax import lax
from jax.experimental import pallas as pl
from jax.experimental.pallas import tpu as pltpu
from jax.sharding import Mesh
from jax.sharding import PartitionSpec as P

HD = 128
SCALE = 1.0 / math.sqrt(HD)
C1 = SCALE * math.log2(math.e)
NEG = -1e30
TILE = 256
PIECES = 4
SEQ = ("y", "z", "c")
YZ = ("y", "z")
CYZ = ("c", "y", "z")
HEAD = ("x", "w")
OWNERS = ("x", "w", "y", "z")
F32 = jnp.float32
BF16 = jnp.bfloat16
SMEM = pl.BlockSpec(memory_space=pltpu.SMEM)
VMEM = pl.BlockSpec(memory_space=pltpu.VMEM)


def dot_nt(a, b):
    return lax.dot_general(a, b, (((1,), (1,)), ((), ())), preferred_element_type=F32)


def dot_nn(a, b):
    return lax.dot_general(a, b, (((1,), (0,)), ((), ())), preferred_element_type=F32)


def dot_tn(a, b):
    return lax.dot_general(a, b, (((0,), (0,)), ((), ())), preferred_element_type=F32)


def span(r):
    return slice(r * TILE, (r + 1) * TILE)


def update(state, s, d):
    m, l, t = state
    s = s.reshape(-1, 8, TILE)
    d = d.reshape(-1, 8, TILE)
    new = jnp.maximum(m, jnp.max(s, axis=0))
    fade = jnp.exp2(m - new)
    w = jnp.exp2(s - new[None])
    return (new, l * fade + jnp.sum(w, axis=0), t * fade + jnp.sum(w * d, axis=0))


def pair_of(kv, j):
    k = jnp.concatenate([kv[2 * j, :HD], kv[2 * j + 1, :HD]], 0)
    v = jnp.concatenate([kv[2 * j, HD : 2 * HD], kv[2 * j + 1, HD : 2 * HD]], 0)
    return k, v


def visible(pos, own, j, shape, key_dim):
    key = lax.broadcasted_iota(jnp.int32, shape, key_dim)
    row = lax.broadcasted_iota(jnp.int32, shape, 1 - key_dim) % HD
    if own:
        return key <= (pos[0] - 2 * j) * HD + row
    return key < (pos[0] + pos[1] - 2 * j) * HD


def sweep_kernel(pos, q, g, mine, other, out):
    tiles = q.shape[0] // TILE

    def step(j, states, masked=False):
        for own, kv in ((True, mine), (False, other)):
            k, v = pair_of(kv, j)
            seen = visible(pos, own, j, (2 * HD, TILE), 0) if masked else None
            new = []
            for r in range(tiles):
                s = dot_nt(k, q[span(r), :]) * C1
                if masked:
                    s = jnp.where(seen, s, NEG)
                new.append(update(states[r], s, dot_nt(v, g[span(r), :])))
            states = tuple(new)
        return states

    zero = jnp.zeros((8, TILE), F32)
    states = tuple((jnp.full((8, TILE), NEG, F32), zero, zero) for _ in range(tiles))
    half = pos[0] // 2
    states = step(half, lax.fori_loop(0, half, step, states), True)
    for r in range(tiles):
        for a in range(3):
            out[a, :, span(r)] = states[r][a]


def prefix_kernel(q, g, pkv, state, grads, stats):
    npre = pkv.shape[1]
    kg = jnp.zeros((npre, HD), F32)
    vg = jnp.zeros((npre, HD), F32)
    for r in range(q.shape[0] // TILE):
        s = dot_nt(pkv[0], q[span(r), :]) * C1
        d = dot_nt(pkv[1], g[span(r), :])
        m, l, t = update(tuple(state[a, :, span(r)] for a in range(3)), s, d)
        top = jnp.max(m, axis=0, keepdims=True)
        fade = jnp.exp2(m - top)
        total = jnp.sum(l * fade, axis=0, keepdims=True)
        delta = jnp.sum(t * fade, axis=0, keepdims=True) / total
        log_total = top + jnp.log2(total)
        stats[0:1, span(r)] = log_total
        stats[1:2, span(r)] = delta
        p = jnp.exp2(s - log_total)
        kg = kg + dot_nn((p * (d - delta)).astype(BF16), q[span(r), :])
        vg = vg + dot_nn(p.astype(BF16), g[span(r), :])
    grads[0] = (kg * SCALE).astype(grads.dtype)
    grads[1] = vg.astype(grads.dtype)


def grad_kernel(piece, pos, q, g, stats, mine, other, extra, out, total, log_total, delta):
    rows = q.shape[0]
    columns = stats[...].T
    log_total[...] = jnp.broadcast_to(columns[:, 0:1], (rows, HD))
    delta[...] = jnp.broadcast_to(columns[:, 1:2], (rows, HD))

    def part(k, v, seen=None):
        for r in range(rows // TILE):
            s = dot_nt(q[span(r), :], k) * C1
            if seen is not None:
                s = jnp.where(seen, s, NEG)
            d = dot_nt(g[span(r), :], v)
            pieces = []
            for b in range(k.shape[0] // HD):
                lanes = slice(b * HD, (b + 1) * HD)
                p = jnp.exp2(s[:, lanes] - log_total[span(r), :])
                pieces.append((p * (d[:, lanes] - delta[span(r), :])).astype(BF16))
            total[span(r), :] += dot_nn(jnp.concatenate(pieces, 1), k)

    def step(i, masked=False):
        for own, kv in ((True, mine), (False, other)):
            k, v = pair_of(kv, i)
            seen = visible(pos, own, first + i, (TILE, 2 * HD), 1) if masked else None
            part(k, v, seen)

    if piece == 0:
        total[...] = jnp.zeros((rows, HD), F32)
        part(extra[0], extra[1])
    else:
        total[...] = extra[...]
    pairs = mine.shape[0] // 2
    first = piece * pairs
    half = pos[0] // 2
    lax.fori_loop(0, jnp.clip(half - first, 0, pairs), lambda i, _: step(i), None)

    @pl.when((half >= first) & (half < first + pairs))
    def _():
        step(half - first, True)

    if piece < PIECES - 1:
        out[...] = total[...]
    else:
        result = (total[...] * SCALE).astype(out.dtype)
        for h in range(rows // HD):
            out[:, h * HD : (h + 1) * HD] = result[h * HD : (h + 1) * HD]


def sweep(pos, q, g, mine, other):
    return pl.pallas_call(
        sweep_kernel,
        out_shape=jax.ShapeDtypeStruct((3, 8, q.shape[0]), F32),
        in_specs=[SMEM] + [VMEM] * 4,
        out_specs=VMEM,
        cost_estimate=pl.CostEstimate(flops=2 * 10**9, bytes_accessed=3 * 10**6, transcendentals=4 * 10**6),
        name="sweep",
    )(pos, q, g, mine, other)


def prefix_part(q, g, pkv, state):
    return pl.pallas_call(
        prefix_kernel,
        out_shape=(
            jax.ShapeDtypeStruct(pkv.shape, BF16),
            jax.ShapeDtypeStruct((2, q.shape[0]), F32),
        ),
        in_specs=[VMEM] * 4,
        out_specs=(VMEM, VMEM),
        cost_estimate=pl.CostEstimate(flops=3 * 10**8, bytes_accessed=10**6, transcendentals=5 * 10**5),
        name="prefix_part",
    )(q, g, pkv, state)


def whole(value):
    return pl.BlockSpec(value.shape, lambda *_: (0,) * value.ndim)


def query_grad_piece(piece, pos, q, g, stats, mine, other, extra):
    n = q.shape[0]
    blocks, *shape = mine.shape
    part = pl.BlockSpec((blocks // PIECES, *shape), lambda *_: (piece, 0, 0))
    out = jax.ShapeDtypeStruct((n, HD), F32)
    if piece == PIECES - 1:
        out = jax.ShapeDtypeStruct((HD, n), BF16)
    return pl.pallas_call(
        functools.partial(grad_kernel, piece),
        out_shape=out,
        in_specs=[SMEM, whole(q), whole(g), whole(stats), part, part, whole(extra)],
        out_specs=whole(out),
        grid=(1,),
        scratch_shapes=[pltpu.VMEM((n, HD), F32)] * 3,
        cost_estimate=pl.CostEstimate(flops=10**9, bytes_accessed=3 * 10**6, transcendentals=10**6),
        name="query_grad",
    )(pos, q, g, stats, mine, other, extra)


def exchange(value, axes):
    return lax.all_to_all(value, axes, 0, 0, tiled=True)


def to_all(value, axes):
    return exchange(jnp.broadcast_to(value, (lax.axis_size(axes), *value.shape)), axes)


def sum_parts(value, axes, dtype=BF16):
    parts = exchange(value.reshape(lax.axis_size(axes), -1, HD).astype(dtype), axes)
    return jnp.sum(parts.astype(F32), axis=0)


def shift(value, axis, steps):
    count = lax.axis_size(axis)
    return lax.ppermute(value, axis, [(i, (i + steps) % count) for i in range(count)])


def by_head(rows):
    return rows.reshape(rows.shape[0], -1, HD).transpose(1, 0, 2).reshape(-1, HD)


def on_device(prefix_embed, w_hidden, b_hidden, w_out, queries, keys, values, out_grad):
    npre, emb = prefix_embed.shape
    units = w_hidden.shape[1]
    core = lax.axis_index("c")
    here = lax.axis_index(YZ)
    head = lax.axis_index(HEAD)
    heads = lax.axis_size(HEAD)
    share = npre // heads
    pos = jnp.stack([here, core]).astype(jnp.int32)

    hidden_pre = jnp.dot(prefix_embed, w_hidden, preferred_element_type=F32) + b_hidden
    tangent = jnp.tanh(hidden_pre)
    hidden = tangent.astype(BF16)
    partial_kv = jnp.einsum("ph,hck->cpk", hidden, w_out, preferred_element_type=F32)
    groups = lax.axis_size(YZ)
    kv = jnp.concatenate([keys, values], 0)
    partial_kv = partial_kv.reshape(groups, -1, HD).astype(BF16)
    mine = exchange(jnp.concatenate([jnp.broadcast_to(kv, (groups, *kv.shape)), partial_kv], 1), YZ)
    own = jnp.sum(mine[:, kv.shape[0] :].astype(F32), axis=0)
    own = (own + shift(own, "c", 1)).astype(BF16)
    other = shift(mine, "c", 1)
    pkv = to_all(own, YZ).reshape(2, npre, HD)
    q = by_head(queries)
    g = by_head(out_grad)
    state = sweep(pos, q, g, mine, other)
    grads, stats = prefix_part(q, g, pkv, state)
    own_grads = sum_parts(grads, SEQ).astype(BF16)
    prefix_grads = to_all(own_grads, SEQ).reshape(2, npre, HD)
    query_grad = pkv
    for piece in range(PIECES):
        query_grad = query_grad_piece(piece, pos, q, g, stats, mine, other, query_grad)
    grad_w_out = jnp.einsum("ph,cpk->hck", hidden, prefix_grads, preferred_element_type=F32)
    hidden_part = jnp.einsum("cpk,hck->ph", prefix_grads, w_out, preferred_element_type=F32)
    parts = exchange(hidden_part.reshape(heads, share, units), HEAD)
    hidden_grad = jnp.sum(parts, axis=0)
    own_tangent = lax.dynamic_slice_in_dim(tangent, head * share, share, 0)
    pre_part = (hidden_grad * (1.0 - own_tangent * own_tangent)).astype(BF16)
    embed_part = dot_nt(pre_part, w_hidden)
    own_embed = sum_parts(embed_part, CYZ).astype(BF16)
    near = to_all(own_embed, OWNERS)
    far = shift(near, "c", 1)
    sides = jnp.stack([jnp.where(core == 0, near, far), jnp.where(core == 0, far, near)], 0)
    sides = sides.reshape(2, heads, -1, emb).transpose(1, 0, 2, 3)
    grad_prefix = sides.reshape(npre, emb).astype(F32)
    both = jnp.concatenate([pre_part, shift(pre_part, "w", 1)], 0)
    lines = lax.axis_size("x")
    pre_rounded = jnp.concatenate([both] + [shift(both, "x", k) for k in range(1, lines)], 0)
    x, w = lax.axis_index("x"), lax.axis_index("w")
    order = []
    for k in range(lines):
        for other_w in (w, 1 - w):
            source = (x - k) % lines * lax.axis_size("w") + other_w
            order.append(lax.dynamic_slice_in_dim(prefix_embed, source * share, share, 0))
    embed_rows = jnp.concatenate(order, 0)
    grad_w_hidden = dot_tn(embed_rows, pre_rounded)
    grad_b_hidden = jnp.sum(pre_rounded.astype(F32), axis=0)
    return (query_grad, grad_w_out, grad_w_hidden, grad_b_hidden, grad_prefix)


def solution(mesh):
    torus = Mesh(mesh.devices.reshape(2, 8, 2, 4, 2), ("y", "z", "c", "x", "w"))
    placed = (
        P(),
        P(None, SEQ),
        P(SEQ),
        P(SEQ, None, HEAD),
        P(SEQ, HEAD),
        P(SEQ, HEAD),
        P(SEQ, HEAD),
        P(SEQ, HEAD),
    )
    return jax.shard_map(
        on_device,
        mesh=torus,
        in_specs=placed,
        out_specs=(P(SEQ, HEAD), P(SEQ, None, HEAD), P(None, SEQ), P(SEQ), P()),
        check_vma=False,
    )
```

time: 196 us -> 178 us (0.908)
  the two profiles are of different devices: /device:TPU:233 before, /device:TPU:1 now
where the time goes in v2:
time: 178 us; the launch traced here: 177 us
  starting transfers between devices  74.8 us (42%)
  waiting for transfers between devices  55.3 us (31%)
  Pallas kernels  20 us (11%)
  local copies, waits for them, and re-layouts  16.8 us (9%)
  matrix products  5.31 us (3%)
  other arithmetic  3.66 us (2%)
    all_to_all x7, starting transfers between devices, exchange(): return lax.all_to_all(value, axes, 0, 0, tiled=True)  61.4 us
    all_to_all x7, waiting for transfers between devices, exchange(): return lax.all_to_all(value, axes, 0, 0, tiled=True)  55.3 us
    ppermute x7, starting transfers between devices, shift(): lax.ppermute(value, axis, [(i, (i + steps) % count) for i in range(count)])  13.4 us
    pallas_call x4, Pallas kernels, query_grad_piece(): pl.pallas_call(functools.partial(grad_kernel, piece), out_shape=out, in_s...  13.4 us
    unnamed x30, local copies, waits for them, and re-layouts  11.2 us
  transfers between devices with their start and end apart: 14, of which 6 were waited for; matrix products, arithmetic and copies ran while one was open for 10% of the time, Pallas kernels for 9%

profile of v2, /device:TPU:1, one launch (start us, length us, event | category | flops | bytes accessed | tf_op | source)
XLA Modules:
  0.0 176.8 jit_solution(17689368783749530853)
XLA Ops:
  1.7 1.3 fusion
  3.5 1.1 pad_maximum_fusion
  4.6 10.3 %all-to-all-start = ((bf16[16,288,128]{2,1,0:T(8,128)(2,1)}), bf16[16,288,128]{2,1,0:T(8,128)(2,1)S(1)}, u32[]{:S(2)}, u32[]{:S(2)}) async-start(bf16[16,288,128]{2,1,0:T(8,128)(2,1)} %pad_maximum_fusion), calls=%async_computation | async-start | bytes 2359296 | tf_op jit(solution)/shard_map/all_to_all | solution.py:212
  14.9 28.1 %all-to-all-done.mine = bf16[16,288,128]{2,1,0:T(8,128)(2,1)S(1)} async-done(((bf16[16,288,128]{2,1,0:T(8,128)(2,1)}), bf16[16,288,128]{2,1,0:T(8,128)(2,1)S(1)}, u32[]{:S(2)}, u32[]{:S(2)}) %all-to-all-start) | async-done | bytes 1179680 | tf_op jit(solution)/shard_map/all_to_all | solution.py:212
  43.0 2.7 %collective-permute-start.1 = (bf16[16,288,128]{2,1,0:T(8,128)(2,1)S(1)}, bf16[16,288,128]{2,1,0:T(8,128)(2,1)S(1)}, u32[]{:S(2)}, u32[]{:S(2)}) collective-permute-start(bf16[16,288,128]{2,1,0:T(8,128)(2,1)S(1)} %all-to-all-done.mine), channel_id=1, source_target_pairs={{0,8},{8,0},{1,9},{9,1},{2,10},{10,2},{3,11},{11,3},{4,12},{12,4},... | collective-permute-start | bytes 3538952 | tf_op jit(solution)/shard_map/ppermute | solution.py:226
  45.7 1.5 dynamic-slice_dynamic-update-slice_fusion.7
  47.2 1.5 dynamic-slice_dynamic-update-slice_fusion.6
  49.4 1.7 copy_bitcast_fusion
  51.2 1.5 dynamic-slice_dynamic-update-slice_fusion.5
  53.4 4.2 %all-to-all-start.1 = ((bf16[16,32,128]{2,1,0:T(8,128)(2,1)}), bf16[16,32,128]{2,1,0:T(8,128)(2,1)S(1)}, u32[]{:S(2)}, u32[]{:S(2)}) async-start(bf16[16,32,128]{2,1,0:T(8,128)(2,1)} %broadcast_in_dim.14), calls=%async_computation.1 | async-start | bytes 262144 | tf_op jit(solution)/shard_map/all_to_all | solution.py:212
  59.3 3.4 %sweep.1.state = f32[3,8,1024]{2,1,0:T(8,128)} custom-call(s32[2]{0:T(128)} %pad_add_fusion.pos, bf16[1024,128]{1,0:T(8,128)(2,1)} %bitcast.51, bf16[1024,128]{1,0:T(8,128)(2,1)} %bitcast.57, bf16[16,288,128]{2,1,0:T(8,128)(2,1)} %copy-done.1, bf16[16,288,128]{2,1,0:T(8,128)(2,1)} %copy-done.2), custom_call_target="tpu_custom_call" | custom-call | flops 2000000000 | bytes 3000000 | tf_op jit(solution)/shard_map/sweep/pallas_call | solution.py:164
  62.6 2.4 %all-to-all-done.1 = bf16[16,32,128]{2,1,0:T(8,128)(2,1)S(1)} async-done(((bf16[16,32,128]{2,1,0:T(8,128)(2,1)}), bf16[16,32,128]{2,1,0:T(8,128)(2,1)S(1)}, u32[]{:S(2)}, u32[]{:S(2)}) %all-to-all-start.1) | async-done | bytes 131104 | tf_op jit(solution)/shard_map/all_to_all | solution.py:212
  65.7 3.2 %prefix_part.1 = (bf16[2,256,128]{2,1,0:T(8,128)(2,1)}, f32[2,1024]{1,0:T(2,128)}) custom-call(bf16[1024,128]{1,0:T(8,128)(2,1)} %bitcast.52, bf16[1024,128]{1,0:T(8,128)(2,1)} %bitcast.58, bf16[2,256,128]{2,1,0:T(8,128)(2,1)} %bitcast.68, f32[3,8,1024]{2,1,0:T(8,128)} %sweep.1.state), custom_call_target="tpu_custom_call" | custom-call | flops 300000000 | bytes 1000000 | tf_op jit(solution)/shard_map/prefix_part/pallas_call | solution.py:175
  68.9 11.5 %all-to-all-start.2 = ((bf16[32,16,128]{2,1,0:T(8,128)(2,1)}), bf16[32,16,128]{2,1,0:T(8,128)(2,1)S(1)}, u32[]{:S(2)}, u32[]{:S(2)}) async-start(bf16[32,16,128]{2,1,0:T(8,128)(2,1)} %bitcast.70), calls=%async_computation.2 | async-start | bytes 262144 | tf_op jit(solution)/shard_map/all_to_all | solution.py:212
  82.3 7.1 %all-to-all-done.2 = bf16[32,16,128]{2,1,0:T(8,128)(2,1)S(1)} async-done(((bf16[32,16,128]{2,1,0:T(8,128)(2,1)}), bf16[32,16,128]{2,1,0:T(8,128)(2,1)S(1)}, u32[]{:S(2)}, u32[]{:S(2)}) %all-to-all-start.2) | async-done | bytes 131104 | tf_op jit(solution)/shard_map/all_to_all | solution.py:212
  90.1 5.2 %all-to-all-start.3 = ((bf16[32,16,128]{2,1,0:T(8,128)(2,1)}), bf16[32,16,128]{2,1,0:T(8,128)(2,1)S(1)}, u32[]{:S(2)}, u32[]{:S(2)}) async-start(bf16[32,16,128]{2,1,0:T(8,128)(2,1)} %broadcast_in_dim.15), calls=%async_computation.3 | async-start | bytes 262144 | tf_op jit(solution)/shard_map/all_to_all | solution.py:212
  96.6 5.0 %query_grad.4.extra = f32[1024,128]{1,0:T(8,128)} custom-call(s32[2]{0:T(128)} %pad_add_fusion.pos, bf16[1024,128]{1,0:T(8,128)(2,1)} %bitcast.53, bf16[1024,128]{1,0:T(8,128)(2,1)} %bitcast.59, f32[2,1024]{1,0:T(2,128)} %get-tuple-element.7.stats, bf16[16,288,128]{2,1,0:T(8,128)(2,1)} %copy-done.1, bf16[16,288,128]{2,1,0:T(8,128)(2,1)} %copy-done.2, ...), custom_call_target="tpu_custom_call" | custom-call | flops 1000000000 | bytes 3000000 | tf_op jit(solution)/shard_map/query_grad/pallas_call | solution.py:199
  101.6 2.8 %all-to-all-done.3 = bf16[32,16,128]{2,1,0:T(8,128)(2,1)S(1)} async-done(((bf16[32,16,128]{2,1,0:T(8,128)(2,1)}), bf16[32,16,128]{2,1,0:T(8,128)(2,1)S(1)}, u32[]{:S(2)}, u32[]{:S(2)}) %all-to-all-start.3) | async-done | bytes 131104 | tf_op jit(solution)/shard_map/all_to_all | solution.py:212
  105.3 6.4 %all-to-all-start.4 = ((f32[8,32,256]{2,1,0:T(8,128)}), f32[8,32,256]{2,1,0:T(8,128)S(1)}, u32[]{:S(2)}, u32[]{:S(2)}) async-start(f32[8,32,256]{2,1,0:T(8,128)} %convolution_bitcast_fusion), calls=%async_computation.4 | async-start | bytes 524288 | tf_op jit(solution)/shard_map/all_to_all | solution.py:212
  111.7 2.9 %query_grad.5.extra = f32[1024,128]{1,0:T(8,128)} custom-call(s32[2]{0:T(128)} %pad_add_fusion.pos, bf16[1024,128]{1,0:T(8,128)(2,1)} %bitcast.54, bf16[1024,128]{1,0:T(8,128)(2,1)} %bitcast.60, f32[2,1024]{1,0:T(2,128)} %get-tuple-element.7.stats, bf16[16,288,128]{2,1,0:T(8,128)(2,1)} %copy-done.1, bf16[16,288,128]{2,1,0:T(8,128)(2,1)} %copy-done.2, ...), custom_call_target="tpu_custom_call" | custom-call | flops 1000000000 | bytes 3000000 | tf_op jit(solution)/shard_map/query_grad/pallas_call | solution.py:199
  114.6 2.8 %query_grad.6.extra = f32[1024,128]{1,0:T(8,128)} custom-call(s32[2]{0:T(128)} %pad_add_fusion.pos, bf16[1024,128]{1,0:T(8,128)(2,1)} %bitcast.55, bf16[1024,128]{1,0:T(8,128)(2,1)} %bitcast.61, f32[2,1024]{1,0:T(2,128)} %get-tuple-element.7.stats, bf16[16,288,128]{2,1,0:T(8,128)(2,1)} %copy-done.1, bf16[16,288,128]{2,1,0:T(8,128)(2,1)} %copy-done.2, ...), custom_call_target="tpu_custom_call" | custom-call | flops 1000000000 | bytes 3000000 | tf_op jit(solution)/shard_map/query_grad/pallas_call | solution.py:199
  117.4 2.7 %query_grad.7 = bf16[128,1024]{1,0:T(8,128)(2,1)} custom-call(s32[2]{0:T(128)} %pad_add_fusion.pos, bf16[1024,128]{1,0:T(8,128)(2,1)} %bitcast.56, bf16[1024,128]{1,0:T(8,128)(2,1)} %bitcast.62, f32[2,1024]{1,0:T(2,128)} %get-tuple-element.7.stats, bf16[16,288,128]{2,1,0:T(8,128)(2,1)} %copy-done.1, bf16[16,288,128]{2,1,0:T(8,128)(2,1)} %copy-done.2, ...), custom_call_target="tpu_custom_call" | custom-call | flops 1000000000 | bytes 3000000 | tf_op jit(solution)/shard_map/query_grad/pallas_call | solution.py:199
  120.2 3.1 %collective-permute-start.2 = (bf16[32,256]{1,0:T(8,128)(2,1)S(1)}, bf16[32,256]{1,0:T(8,128)(2,1)S(1)}, u32[]{:S(2)}, u32[]{:S(2)}) collective-permute-start(bf16[32,256]{1,0:T(8,128)(2,1)S(1)} %get-tuple-element.15), channel_id=1, source_target_pairs={{0,1},{1,0},{2,3},{3,2},{4,5},{5,4},{6,7},{7,6},{8,9},{9,8},{10,11... | collective-permute-start | bytes 49160 | tf_op jit(solution)/shard_map/ppermute | solution.py:226
  124.1 16.5 %all-to-all-start.5 = ((bf16[32,8,128]{2,1,0:T(8,128)(2,1)}), bf16[32,8,128]{2,1,0:T(8,128)(2,1)S(1)}, u32[]{:S(2)}, u32[]{:S(2)}) async-start(bf16[32,8,128]{2,1,0:T(8,128)(2,1)} %bitcast.30), calls=%async_computation.5 | async-start | bytes 131072 | tf_op jit(solution)/shard_map/all_to_all | solution.py:212
  141.7 1.2 collective-permute-start.3
  142.9 2.4 %collective-permute-start.4 = (bf16[64,256]{1,0:T(8,128)(2,1)S(1)}, bf16[64,256]{1,0:T(8,128)(2,1)S(1)}, u32[]{:S(2)}, u32[]{:S(2)}) collective-permute-start(bf16[64,256]{1,0:T(8,128)(2,1)S(1)} %pad_maximum_fusion.2), channel_id=1, source_target_pairs={{0,4},{2,6},{4,0},{6,2},{1,5},{3,7},{5,1},{7,3},{8,12},{10,14},{12... | collective-permute-start | bytes 98312 | tf_op jit(solution)/shard_map/ppermute | solution.py:226
  145.3 1.2 collective-permute-start.5
  146.5 2.3 %all-to-all-done.5 = bf16[32,8,128]{2,1,0:T(8,128)(2,1)S(1)} async-done(((bf16[32,8,128]{2,1,0:T(8,128)(2,1)}), bf16[32,8,128]{2,1,0:T(8,128)(2,1)S(1)}, u32[]{:S(2)}, u32[]{:S(2)}) %all-to-all-start.5) | async-done | bytes 65568 | tf_op jit(solution)/shard_map/all_to_all | solution.py:212
  149.6 7.4 %all-to-all-start.6 = ((bf16[128,8,128]{2,1,0:T(8,128)(2,1)}), bf16[128,8,128]{2,1,0:T(8,128)(2,1)S(1)}, u32[]{:S(2)}, u32[]{:S(2)}) async-start(bf16[128,8,128]{2,1,0:T(8,128)(2,1)} %broadcast_in_dim.16), calls=%async_computation.6 | async-start | bytes 524288 | tf_op jit(solution)/shard_map/all_to_all | solution.py:212
  157.7 12.6 %all-to-all-done.6 = bf16[128,8,128]{2,1,0:T(8,128)(2,1)S(1)} async-done(((bf16[128,8,128]{2,1,0:T(8,128)(2,1)}), bf16[128,8,128]{2,1,0:T(8,128)(2,1)S(1)}, u32[]{:S(2)}, u32[]{:S(2)}) %all-to-all-start.6) | async-done | bytes 262176 | tf_op jit(solution)/shard_map/all_to_all | solution.py:212
  170.3 2.8 %collective-permute-start.6 = (bf16[128,8,128]{2,1,0:T(8,128)(2,1)S(1)}, bf16[128,8,128]{2,1,0:T(8,128)(2,1)S(1)}, u32[]{:S(2)}, u32[]{:S(2)}) collective-permute-start(bf16[128,8,128]{2,1,0:T(8,128)(2,1)S(1)} %all-to-all-done.6), channel_id=1, source_target_pairs={{0,8},{8,0},{1,9},{9,1},{2,10},{10,2},{3,11},{11,3},{4,12},{12,4},... | collective-permute-start | bytes 786440 | tf_op jit(solution)/shard_map/ppermute | solution.py:226
  173.0 2.4 %fusion.9 = f32[1024,256]{1,0:T(8,128)} fusion(bf16[256,1024]{1,0:T(8,128)(2,1)} %dynamic-slice_dynamic-update-slice_fusion, bf16[256,256]{1,0:T(8,128)(2,1)S(1)} %constant_dynamic-update-slice_fusion), kind=kOutput, calls=%fused_computation.39 | convolution fusion | flops 134217728 | bytes 1703936 | tf_op jit(solution)/shard_map/dot_general | solution.py:38
  (61 shorter events, 15.0 us)
Async XLA Ops:
  0.6 1.0 copy-start
  0.6 2.4 %copy-start.4 = (bf16[256,2,128]{2,1,0:T(2,128)(2,1)S(1)}, bf16[256,2,128]{2,1,0:T(2,128)(2,1)}, u32[]{:S(2)}) copy-start(bf16[256,2,128]{2,1,0:T(2,128)(2,1)} %param.11) | copy-start | bytes 393220
  0.7 2.6 %copy-start.7 = (bf16[128,128]{1,0:T(8,128)(2,1)S(1)}, bf16[128,128]{1,0:T(8,128)(2,1)}, u32[]{:S(2)}) copy-start(bf16[128,128]{1,0:T(8,128)(2,1)} %param.14) | copy-start | bytes 98308
  0.7 2.6 %copy-start.8 = (bf16[128,128]{1,0:T(8,128)(2,1)S(1)}, bf16[128,128]{1,0:T(8,128)(2,1)}, u32[]{:S(2)}) copy-start(bf16[128,128]{1,0:T(8,128)(2,1)} %param.13) | copy-start | bytes 98308
  4.6 44.0 %copy-start.5 = (bf16[128,1024]{1,0:T(8,128)(2,1)S(1)}, bf16[128,1024]{1,0:T(8,128)(2,1)}, u32[]{:S(2)}) copy-start(bf16[128,1024]{1,0:T(8,128)(2,1)} %param.12) | copy-start | bytes 786436
  4.6 38.4 %all-to-all-start = ((bf16[16,288,128]{2,1,0:T(8,128)(2,1)}), bf16[16,288,128]{2,1,0:T(8,128)(2,1)S(1)}, u32[]{:S(2)}, u32[]{:S(2)}) async-start(bf16[16,288,128]{2,1,0:T(8,128)(2,1)} %pad_maximum_fusion), calls=%async_computation | async-start | bytes 2359296 | tf_op jit(solution)/shard_map/all_to_all | solution.py:212
  43.0 15.3 %copy-start.1 = (bf16[16,288,128]{2,1,0:T(8,128)(2,1)}, bf16[16,288,128]{2,1,0:T(8,128)(2,1)S(1)}, u32[]{:S(2)}) copy-start(bf16[16,288,128]{2,1,0:T(8,128)(2,1)S(1)} %all-to-all-done.mine) | copy-start | bytes 3538948
  43.0 15.3 %collective-permute-start.1 = (bf16[16,288,128]{2,1,0:T(8,128)(2,1)S(1)}, bf16[16,288,128]{2,1,0:T(8,128)(2,1)S(1)}, u32[]{:S(2)}, u32[]{:S(2)}) collective-permute-start(bf16[16,288,128]{2,1,0:T(8,128)(2,1)S(1)} %all-to-all-done.mine), channel_id=1, source_target_pairs={{0,8},{8,0},{1,9},{9,1},{2,10},{10,2},{3,11},{11,3},{4,12},{12,4},... | collective-permute-start | bytes 3538952 | tf_op jit(solution)/shard_map/ppermute | solution.py:226
  51.1 1.6 collective-permute-start
  53.4 11.6 %all-to-all-start.1 = ((bf16[16,32,128]{2,1,0:T(8,128)(2,1)}), bf16[16,32,128]{2,1,0:T(8,128)(2,1)S(1)}, u32[]{:S(2)}, u32[]{:S(2)}) async-start(bf16[16,32,128]{2,1,0:T(8,128)(2,1)} %broadcast_in_dim.14), calls=%async_computation.1 | async-start | bytes 262144 | tf_op jit(solution)/shard_map/all_to_all | solution.py:212
  58.3 1.0 copy-start.2
  62.6 17.8 %copy-start.3 = (bf16[256,1024]{1,0:T(8,128)(2,1)S(1)}, bf16[256,1024]{1,0:T(8,128)(2,1)}, u32[]{:S(2)}) copy-start(bf16[256,1024]{1,0:T(8,128)(2,1)} %param.8) | copy-start | bytes 1572868
  65.0 0.7 copy-start.6
  68.9 20.5 %all-to-all-start.2 = ((bf16[32,16,128]{2,1,0:T(8,128)(2,1)}), bf16[32,16,128]{2,1,0:T(8,128)(2,1)S(1)}, u32[]{:S(2)}, u32[]{:S(2)}) async-start(bf16[32,16,128]{2,1,0:T(8,128)(2,1)} %bitcast.70), calls=%async_computation.2 | async-start | bytes 262144 | tf_op jit(solution)/shard_map/all_to_all | solution.py:212
  90.1 14.3 %all-to-all-start.3 = ((bf16[32,16,128]{2,1,0:T(8,128)(2,1)}), bf16[32,16,128]{2,1,0:T(8,128)(2,1)S(1)}, u32[]{:S(2)}, u32[]{:S(2)}) async-start(bf16[32,16,128]{2,1,0:T(8,128)(2,1)} %broadcast_in_dim.15), calls=%async_computation.3 | async-start | bytes 262144 | tf_op jit(solution)/shard_map/all_to_all | solution.py:212
  105.3 14.8 %all-to-all-start.4 = ((f32[8,32,256]{2,1,0:T(8,128)}), f32[8,32,256]{2,1,0:T(8,128)S(1)}, u32[]{:S(2)}, u32[]{:S(2)}) async-start(f32[8,32,256]{2,1,0:T(8,128)} %convolution_bitcast_fusion), calls=%async_computation.4 | async-start | bytes 524288 | tf_op jit(solution)/shard_map/all_to_all | solution.py:212
  120.2 21.6 %collective-permute-start.2 = (bf16[32,256]{1,0:T(8,128)(2,1)S(1)}, bf16[32,256]{1,0:T(8,128)(2,1)S(1)}, u32[]{:S(2)}, u32[]{:S(2)}) collective-permute-start(bf16[32,256]{1,0:T(8,128)(2,1)S(1)} %get-tuple-element.15), channel_id=1, source_target_pairs={{0,1},{1,0},{2,3},{3,2},{4,5},{5,4},{6,7},{7,6},{8,9},{9,8},{10,11... | collective-permute-start | bytes 49160 | tf_op jit(solution)/shard_map/ppermute | solution.py:226
  124.1 24.7 %all-to-all-start.5 = ((bf16[32,8,128]{2,1,0:T(8,128)(2,1)}), bf16[32,8,128]{2,1,0:T(8,128)(2,1)S(1)}, u32[]{:S(2)}, u32[]{:S(2)}) async-start(bf16[32,8,128]{2,1,0:T(8,128)(2,1)} %bitcast.30), calls=%async_computation.5 | async-start | bytes 131072 | tf_op jit(solution)/shard_map/all_to_all | solution.py:212
  141.7 15.3 %collective-permute-start.3 = (bf16[64,256]{1,0:T(8,128)(2,1)S(1)}, bf16[64,256]{1,0:T(8,128)(2,1)S(1)}, u32[]{:S(2)}, u32[]{:S(2)}) collective-permute-start(bf16[64,256]{1,0:T(8,128)(2,1)S(1)} %pad_maximum_fusion.2), channel_id=1, source_target_pairs={{0,2},{2,4},{4,6},{6,0},{1,3},{3,5},{5,7},{7,1},{8,10},{10,12},{12... | collective-permute-start | bytes 98312 | tf_op jit(solution)/shard_map/ppermute | solution.py:226
  142.9 14.1 %collective-permute-start.4 = (bf16[64,256]{1,0:T(8,128)(2,1)S(1)}, bf16[64,256]{1,0:T(8,128)(2,1)S(1)}, u32[]{:S(2)}, u32[]{:S(2)}) collective-permute-start(bf16[64,256]{1,0:T(8,128)(2,1)S(1)} %pad_maximum_fusion.2), channel_id=1, source_target_pairs={{0,4},{2,6},{4,0},{6,2},{1,5},{3,7},{5,1},{7,3},{8,12},{10,14},{12... | collective-permute-start | bytes 98312 | tf_op jit(solution)/shard_map/ppermute | solution.py:226
  145.3 11.8 %collective-permute-start.5 = (bf16[64,256]{1,0:T(8,128)(2,1)S(1)}, bf16[64,256]{1,0:T(8,128)(2,1)S(1)}, u32[]{:S(2)}, u32[]{:S(2)}) collective-permute-start(bf16[64,256]{1,0:T(8,128)(2,1)S(1)} %pad_maximum_fusion.2), channel_id=1, source_target_pairs={{0,6},{2,0},{4,2},{6,4},{1,7},{3,1},{5,3},{7,5},{8,14},{10,8},{12,... | collective-permute-start | bytes 98312 | tf_op jit(solution)/shard_map/ppermute | solution.py:226
  149.6 20.7 %all-to-all-start.6 = ((bf16[128,8,128]{2,1,0:T(8,128)(2,1)}), bf16[128,8,128]{2,1,0:T(8,128)(2,1)S(1)}, u32[]{:S(2)}, u32[]{:S(2)}) async-start(bf16[128,8,128]{2,1,0:T(8,128)(2,1)} %broadcast_in_dim.16), calls=%async_computation.6 | async-start | bytes 524288 | tf_op jit(solution)/shard_map/all_to_all | solution.py:212
  170.3 5.1 %collective-permute-start.6 = (bf16[128,8,128]{2,1,0:T(8,128)(2,1)S(1)}, bf16[128,8,128]{2,1,0:T(8,128)(2,1)S(1)}, u32[]{:S(2)}, u32[]{:S(2)}) collective-permute-start(bf16[128,8,128]{2,1,0:T(8,128)(2,1)S(1)} %all-to-all-done.6), channel_id=1, source_target_pairs={{0,8},{8,0},{1,9},{9,1},{2,10},{10,2},{3,11},{11,3},{4,12},{12,4},... | collective-permute-start | bytes 786440 | tf_op jit(solution)/shard_map/ppermute | solution.py:226

commit v3 on v2

--- a/solution.py
+++ b/solution.py
@@ -206,6 +206,33 @@
         cost_estimate=pl.CostEstimate(flops=10**9, bytes_accessed=3 * 10**6, transcendentals=10**6),
         name="query_grad",
     )(pos, q, g, stats, mine, other, extra)
+
+
+def w_hidden_kernel(place, embed, *refs):
+    *parts, grad_w, grad_b, pre = refs
+    lines = len(parts)
+    share = parts[0].shape[0] // 2
+    for k, part in enumerate(parts):
+        line = (place[0] + lines - k) % lines
+        for side in range(2):
+            source = 2 * line + (place[1] + side) % 2
+            pre[pl.ds(pl.multiple_of(source * share, share), share), :] = part[side * share : (side + 1) * share]
+    grad_w[...] = dot_tn(embed[...], pre[...])
+    grad_b[...] = jnp.sum(pre[...].astype(F32), axis=0)
+
+
+def w_hidden_grad(place, embed, *parts):
+    npre, emb = embed.shape
+    units = parts[0].shape[1]
+    return pl.pallas_call(
+        w_hidden_kernel,
+        out_shape=(jax.ShapeDtypeStruct((emb, units), F32), jax.ShapeDtypeStruct((units,), F32)),
+        in_specs=[SMEM] + [VMEM] * (1 + len(parts)),
+        out_specs=(VMEM, VMEM),
+        scratch_shapes=[pltpu.VMEM((npre, units), BF16)],
+        cost_estimate=pl.CostEstimate(flops=2 * 10**8, bytes_accessed=2 * 10**6, transcendentals=0),
+        name="w_hidden_grad",
+    )(place, embed, *parts)
 
 
 def exchange(value, axes):
@@ -275,17 +302,9 @@
     sides = sides.reshape(2, heads, -1, emb).transpose(1, 0, 2, 3)
     grad_prefix = sides.reshape(npre, emb).astype(F32)
     both = jnp.concatenate([pre_part, shift(pre_part, "w", 1)], 0)
-    lines = lax.axis_size("x")
-    pre_rounded = jnp.concatenate([both] + [shift(both, "x", k) for k in range(1, lines)], 0)
-    x, w = lax.axis_index("x"), lax.axis_index("w")
-    order = []
-    for k in range(lines):
-        for other_w in (w, 1 - w):
-            source = (x - k) % lines * lax.axis_size("w") + other_w
-            order.append(lax.dynamic_slice_in_dim(prefix_embed, source * share, share, 0))
-    embed_rows = jnp.concatenate(order, 0)
-    grad_w_hidden = dot_tn(embed_rows, pre_rounded)
-    grad_b_hidden = jnp.sum(pre_rounded.astype(F32), axis=0)
+    turns = [shift(both, "x", k) for k in range(1, lax.axis_size("x"))]
+    place = jnp.stack([lax.axis_index("x"), lax.axis_index("w")]).astype(jnp.int32)
+    grad_w_hidden, grad_b_hidden = w_hidden_grad(place, prefix_embed, both, *turns)
     return (query_grad, grad_w_out, grad_w_hidden, grad_b_hidden, grad_prefix)
 
 

time: 178 us -> 172 us (0.966)
  the two profiles are of different devices: /device:TPU:1 before, /device:TPU:233 now
where the time goes in v3:
time: 172 us; the launch traced here: 170 us
  blocking collectives  74.5 us (43%)
  Pallas kernels  40.6 us (24%)
  starting transfers between devices  31 us (18%)
  waiting for transfers between devices  9.69 us (6%)
  local copies, waits for them, and re-layouts  7.65 us (4%)
  matrix products  2.93 us (2%)
  other arithmetic  2.46 us (1%)
    all_to_all x4, blocking collectives, exchange(): return lax.all_to_all(value, axes, 0, 0, tiled=True)  74.5 us
    pallas_call x4, Pallas kernels, query_grad_piece(): pl.pallas_call(functools.partial(grad_kernel, piece), out_shape=out, in_s...  25.8 us
    all_to_all x3, starting transfers between devices, exchange(): return lax.all_to_all(value, axes, 0, 0, tiled=True)  19.9 us
    ppermute x7, starting transfers between devices, shift(): lax.ppermute(value, axis, [(i, (i + steps) % count) for i in range(count)])  11.1 us
    pallas_call x1, Pallas kernels, sweep(): pl.pallas_call(sweep_kernel, out_shape=jax.ShapeDtypeStruct((3, 8, q.shap...  9.21 us
    all_to_all x3, waiting for transfers between devices, exchange(): return lax.all_to_all(value, axes, 0, 0, tiled=True)  8.25 us
    unnamed x28, local copies, waits for them, and re-layouts  4.26 us
  transfers between devices with their start and end apart: 10, of which 3 were waited for; matrix products, arithmetic and copies ran while one was open for 3% of the time, Pallas kernels for 22%

profile of v3, /device:TPU:233, one launch (start us, length us, event | category | flops | bytes accessed | tf_op | source)
XLA Modules:
  0.0 169.7 jit_solution(17441695834996264459)
XLA Ops:
  0.7 1.0 copy-done
  1.7 1.3 fusion
  3.6 34.0 %all_to_all.35.mine = bf16[16,288,128]{2,1,0:T(8,128)(2,1)S(1)} all-to-all(bf16[16,288,128]{2,1,0:T(8,128)(2,1)S(1)} %pad_maximum_fusion), channel_id=1, replica_groups=mesh['y'=2,'z'=8,'c'=2,'x'=4,'w'=2] {'y','z'}, dimensions={0} | all-to-all | bytes 2359296 | tf_op jit(solution)/shard_map/all_to_all | solution.py:239
  37.6 2.1 %collective-permute-start.1 = (bf16[16,288,128]{2,1,0:T(8,128)(2,1)S(1)}, bf16[16,288,128]{2,1,0:T(8,128)(2,1)S(1)}, u32[]{:S(2)}, u32[]{:S(2)}) collective-permute-start(bf16[16,288,128]{2,1,0:T(8,128)(2,1)S(1)} %all_to_all.35.mine), channel_id=1, source_target_pairs={{0,8},{8,0},{1,9},{9,1},{2,10},{10,2},{3,11},{11,3},{4,12},{12,4},... | collective-permute-start | bytes 3538952 | tf_op jit(solution)/shard_map/ppermute | solution.py:253
  39.7 0.8 copy_bitcast_fusion.1
  40.7 0.8 copy_bitcast_fusion
  41.4 0.8 collective-permute-done
  42.2 0.7 broadcast_in_dim.14
  42.9 5.6 %all-to-all-start.1 = ((bf16[16,32,128]{2,1,0:T(8,128)(2,1)}), bf16[16,32,128]{2,1,0:T(8,128)(2,1)S(1)}, u32[]{:S(2)}, u32[]{:S(2)}) async-start(bf16[16,32,128]{2,1,0:T(8,128)(2,1)} %broadcast_in_dim.14), calls=%async_computation.1 | async-start | bytes 262144 | tf_op jit(solution)/shard_map/all_to_all | solution.py:239
  49.0 1.0 copy-done.2
  50.0 9.2 %sweep.1.state = f32[3,8,1024]{2,1,0:T(8,128)} custom-call(s32[2]{0:T(128)} %pad_add_fusion.pos, bf16[1024,128]{1,0:T(8,128)(2,1)} %bitcast.51, bf16[1024,128]{1,0:T(8,128)(2,1)} %bitcast.57, bf16[16,288,128]{2,1,0:T(8,128)(2,1)} %copy-done.1, bf16[16,288,128]{2,1,0:T(8,128)(2,1)} %copy-done.2), custom_call_target="tpu_custom_call" | custom-call | flops 2000000000 | bytes 3000000 | tf_op jit(solution)/shard_map/sweep/pallas_call | solution.py:164
  59.9 3.2 %prefix_part.1 = (bf16[2,256,128]{2,1,0:T(8,128)(2,1)}, f32[2,1024]{1,0:T(2,128)}) custom-call(bf16[1024,128]{1,0:T(8,128)(2,1)} %bitcast.52, bf16[1024,128]{1,0:T(8,128)(2,1)} %bitcast.58, bf16[2,256,128]{2,1,0:T(8,128)(2,1)} %bitcast.69, f32[3,8,1024]{2,1,0:T(8,128)} %sweep.1.state), custom_call_target="tpu_custom_call" | custom-call | flops 300000000 | bytes 1000000 | tf_op jit(solution)/shard_map/prefix_part/pallas_call | solution.py:175
  63.1 14.2 %all_to_all.36 = bf16[32,16,128]{2,1,0:T(8,128)(2,1)S(1)} all-to-all(bf16[32,16,128]{2,1,0:T(8,128)(2,1)} %bitcast.71), channel_id=1, replica_groups=mesh['y'=2,'z'=8,'c'=2,'x'=4,'w'=2] {'y','z','c'}, dimensions={0} | all-to-all | bytes 262144 | tf_op jit(solution)/shard_map/all_to_all | solution.py:239
  77.4 13.3 %all_to_all.37 = bf16[32,16,128]{2,1,0:T(8,128)(2,1)S(1)} all-to-all(bf16[32,16,128]{2,1,0:T(8,128)(2,1)S(1)} %broadcast_in_dim.15), channel_id=1, replica_groups=mesh['y'=2,'z'=8,'c'=2,'x'=4,'w'=2] {'y','z','c'}, dimensions={0} | all-to-all | bytes 262144 | tf_op jit(solution)/shard_map/all_to_all | solution.py:239
  90.7 0.9 convolution_bitcast_fusion
  91.6 5.7 %all-to-all-start.4 = ((f32[8,32,256]{2,1,0:T(8,128)}), f32[8,32,256]{2,1,0:T(8,128)S(1)}, u32[]{:S(2)}, u32[]{:S(2)}) async-start(f32[8,32,256]{2,1,0:T(8,128)} %convolution_bitcast_fusion), calls=%async_computation.4 | async-start | bytes 524288 | tf_op jit(solution)/shard_map/all_to_all | solution.py:239
  97.4 8.2 %all-to-all-done.4 = f32[8,32,256]{2,1,0:T(8,128)S(1)} async-done(((f32[8,32,256]{2,1,0:T(8,128)}), f32[8,32,256]{2,1,0:T(8,128)S(1)}, u32[]{:S(2)}, u32[]{:S(2)}) %all-to-all-start.4) | async-done | bytes 262176 | tf_op jit(solution)/shard_map/all_to_all | solution.py:239
  106.0 13.0 %all_to_all.38 = bf16[32,8,128]{2,1,0:T(8,128)(2,1)S(1)} all-to-all(bf16[32,8,128]{2,1,0:T(8,128)(2,1)S(1)} %bitcast.68), channel_id=1, replica_groups=mesh['y'=2,'z'=8,'c'=2,'x'=4,'w'=2] {'c','y','z'}, dimensions={0} | all-to-all | bytes 131072 | tf_op jit(solution)/shard_map/all_to_all | solution.py:239
  119.0 0.8 broadcast_in_dim.16
  119.8 8.6 %all-to-all-start.6 = ((bf16[128,8,128]{2,1,0:T(8,128)(2,1)}), bf16[128,8,128]{2,1,0:T(8,128)(2,1)S(1)}, u32[]{:S(2)}, u32[]{:S(2)}) async-start(bf16[128,8,128]{2,1,0:T(8,128)(2,1)} %broadcast_in_dim.16), calls=%async_computation.6 | async-start | bytes 524288 | tf_op jit(solution)/shard_map/all_to_all | solution.py:239
  129.0 6.9 %query_grad.4.extra = f32[1024,128]{1,0:T(8,128)} custom-call(s32[2]{0:T(128)} %pad_add_fusion.pos, bf16[1024,128]{1,0:T(8,128)(2,1)} %bitcast.53, bf16[1024,128]{1,0:T(8,128)(2,1)} %bitcast.59, f32[2,1024]{1,0:T(2,128)} %get-tuple-element.9.stats, bf16[16,288,128]{2,1,0:T(8,128)(2,1)} %copy-done.1, bf16[16,288,128]{2,1,0:T(8,128)(2,1)} %copy-done.2, ...), custom_call_target="tpu_custom_call" | custom-call | flops 1000000000 | bytes 3000000 | tf_op jit(solution)/shard_map/query_grad/pallas_call | solution.py:199
  135.9 6.3 %query_grad.5.extra = f32[1024,128]{1,0:T(8,128)} custom-call(s32[2]{0:T(128)} %pad_add_fusion.pos, bf16[1024,128]{1,0:T(8,128)(2,1)} %bitcast.54, bf16[1024,128]{1,0:T(8,128)(2,1)} %bitcast.60, f32[2,1024]{1,0:T(2,128)} %get-tuple-element.9.stats, bf16[16,288,128]{2,1,0:T(8,128)(2,1)} %copy-done.1, bf16[16,288,128]{2,1,0:T(8,128)(2,1)} %copy-done.2, ...), custom_call_target="tpu_custom_call" | custom-call | flops 1000000000 | bytes 3000000 | tf_op jit(solution)/shard_map/query_grad/pallas_call | solution.py:199
  142.2 6.3 %query_grad.6.extra = f32[1024,128]{1,0:T(8,128)} custom-call(s32[2]{0:T(128)} %pad_add_fusion.pos, bf16[1024,128]{1,0:T(8,128)(2,1)} %bitcast.55, bf16[1024,128]{1,0:T(8,128)(2,1)} %bitcast.61, f32[2,1024]{1,0:T(2,128)} %get-tuple-element.9.stats, bf16[16,288,128]{2,1,0:T(8,128)(2,1)} %copy-done.1, bf16[16,288,128]{2,1,0:T(8,128)(2,1)} %copy-done.2, ...), custom_call_target="tpu_custom_call" | custom-call | flops 1000000000 | bytes 3000000 | tf_op jit(solution)/shard_map/query_grad/pallas_call | solution.py:199
  148.5 1.9 %collective-permute-start.2 = (bf16[32,256]{1,0:T(8,128)(2,1)S(1)}, bf16[32,256]{1,0:T(8,128)(2,1)S(1)}, u32[]{:S(2)}, u32[]{:S(2)}) collective-permute-start(bf16[32,256]{1,0:T(8,128)(2,1)S(1)} %multiply_convert_fusion), channel_id=1, source_target_pairs={{0,1},{1,0},{2,3},{3,2},{4,5},{5,4},{6,7},{7,6},{8,9},{9,8},{10,11... | collective-permute-start | bytes 49160 | tf_op jit(solution)/shard_map/ppermute | solution.py:253
  150.4 6.3 %query_grad.7 = bf16[128,1024]{1,0:T(8,128)(2,1)} custom-call(s32[2]{0:T(128)} %pad_add_fusion.pos, bf16[1024,128]{1,0:T(8,128)(2,1)} %bitcast.56, bf16[1024,128]{1,0:T(8,128)(2,1)} %bitcast.62, f32[2,1024]{1,0:T(2,128)} %get-tuple-element.9.stats, bf16[16,288,128]{2,1,0:T(8,128)(2,1)} %copy-done.1, bf16[16,288,128]{2,1,0:T(8,128)(2,1)} %copy-done.2, ...), custom_call_target="tpu_custom_call" | custom-call | flops 1000000000 | bytes 3000000 | tf_op jit(solution)/shard_map/query_grad/pallas_call | solution.py:199
  156.7 1.4 collective-permute-start.6
  158.1 1.7 %collective-permute-start.3 = (bf16[64,256]{1,0:T(8,128)(2,1)S(1)}, bf16[64,256]{1,0:T(8,128)(2,1)S(1)}, u32[]{:S(2)}, u32[]{:S(2)}) collective-permute-start(bf16[64,256]{1,0:T(8,128)(2,1)S(1)} %pad_maximum_fusion.2.refs_0_), channel_id=1, source_target_pairs={{0,2},{2,4},{4,6},{6,0},{1,3},{3,5},{5,7},{7,1},{8,10},{10,12},{12... | collective-permute-start | bytes 98312 | tf_op jit(solution)/shard_map/ppermute | solution.py:253
  159.8 2.8 %collective-permute-start.4 = (bf16[64,256]{1,0:T(8,128)(2,1)S(1)}, bf16[64,256]{1,0:T(8,128)(2,1)S(1)}, u32[]{:S(2)}, u32[]{:S(2)}) collective-permute-start(bf16[64,256]{1,0:T(8,128)(2,1)S(1)} %pad_maximum_fusion.2.refs_0_), channel_id=1, source_target_pairs={{0,4},{2,6},{4,0},{6,2},{1,5},{3,7},{5,1},{7,3},{8,12},{10,14},{12... | collective-permute-start | bytes 98312 | tf_op jit(solution)/shard_map/ppermute | solution.py:253
  162.6 1.0 collective-permute-start.5
  163.8 0.9 copy.19
  166.0 2.4 %w_hidden_grad.1 = (f32[1024,256]{1,0:T(8,128)}, f32[256]{0:T(256)}) custom-call(s32[2]{0:T(128)} %pad_add_fusion.1.place, bf16[256,1024]{1,0:T(8,128)(2,1)} %embed.1, bf16[64,256]{1,0:T(8,128)(2,1)} %copy-done.7, bf16[64,256]{1,0:T(8,128)(2,1)} %copy-done.10, bf16[64,256]{1,0:T(8,128)(2,1)} %copy-done.11, bf16[64,256]{1,0:T(8,128)(2,1)} %copy-done.12), custom_call_target="tpu_custom_call" | custom-call | flops 200000000 | bytes 2000000 | tf_op jit(solution)/shard_map/w_hidden_grad/pallas_call | solution.py:227
  168.7 1.0 maximum_convert_fusion
  (53 shorter events, 4.7 us)
Async XLA Ops:
  0.6 1.0 copy-start
  0.6 2.4 %copy-start.3 = (bf16[256,2,128]{2,1,0:T(2,128)(2,1)S(1)}, bf16[256,2,128]{2,1,0:T(2,128)(2,1)}, u32[]{:S(2)}) copy-start(bf16[256,2,128]{2,1,0:T(2,128)(2,1)} %param.11) | copy-start | bytes 393220
  0.7 2.6 %copy-start.8 = (bf16[128,128]{1,0:T(8,128)(2,1)S(1)}, bf16[128,128]{1,0:T(8,128)(2,1)}, u32[]{:S(2)}) copy-start(bf16[128,128]{1,0:T(8,128)(2,1)} %param.14) | copy-start | bytes 98308
  0.7 2.6 %copy-start.9 = (bf16[128,128]{1,0:T(8,128)(2,1)S(1)}, bf16[128,128]{1,0:T(8,128)(2,1)}, u32[]{:S(2)}) copy-start(bf16[128,128]{1,0:T(8,128)(2,1)} %param.13) | copy-start | bytes 98308
  3.6 36.2 %copy-start.4 = (bf16[128,1024]{1,0:T(8,128)(2,1)S(1)}, bf16[128,1024]{1,0:T(8,128)(2,1)}, u32[]{:S(2)}) copy-start(bf16[128,1024]{1,0:T(8,128)(2,1)} %param.12) | copy-start | bytes 786436
  3.6 37.1 %copy-start.5 = (bf16[128,1024]{1,0:T(8,128)(2,1)S(1)}, bf16[128,1024]{1,0:T(8,128)(2,1)}, u32[]{:S(2)}) copy-start(bf16[128,1024]{1,0:T(8,128)(2,1)} %param.15) | copy-start | bytes 786436
  37.6 11.4 %copy-start.1 = (bf16[16,288,128]{2,1,0:T(8,128)(2,1)}, bf16[16,288,128]{2,1,0:T(8,128)(2,1)S(1)}, u32[]{:S(2)}) copy-start(bf16[16,288,128]{2,1,0:T(8,128)(2,1)S(1)} %all_to_all.35.mine) | copy-start | bytes 3538948
  37.6 11.4 %collective-permute-start.1 = (bf16[16,288,128]{2,1,0:T(8,128)(2,1)S(1)}, bf16[16,288,128]{2,1,0:T(8,128)(2,1)S(1)}, u32[]{:S(2)}, u32[]{:S(2)}) collective-permute-start(bf16[16,288,128]{2,1,0:T(8,128)(2,1)S(1)} %all_to_all.35.mine), channel_id=1, source_target_pairs={{0,8},{8,0},{1,9},{9,1},{2,10},{10,2},{3,11},{11,3},{4,12},{12,4},... | collective-permute-start | bytes 3538952 | tf_op jit(solution)/shard_map/ppermute | solution.py:253
  40.5 1.7 %collective-permute-start = (f32[32,128]{1,0:T(8,128)S(1)}, f32[32,128]{1,0:T(8,128)S(1)}, u32[]{:S(2)}, u32[]{:S(2)}) collective-permute-start(f32[32,128]{1,0:T(8,128)S(1)} %convert_reduce_fusion), channel_id=1, source_target_pairs={{0,8},{8,0},{1,9},{9,1},{2,10},{10,2},{3,11},{11,3},{4,12},{12,4},... | collective-permute-start | bytes 49160 | tf_op jit(solution)/shard_map/ppermute | solution.py:253
  42.9 16.4 %all-to-all-start.1 = ((bf16[16,32,128]{2,1,0:T(8,128)(2,1)}), bf16[16,32,128]{2,1,0:T(8,128)(2,1)S(1)}, u32[]{:S(2)}, u32[]{:S(2)}) async-start(bf16[16,32,128]{2,1,0:T(8,128)(2,1)} %broadcast_in_dim.14), calls=%async_computation.1 | async-start | bytes 262144 | tf_op jit(solution)/shard_map/all_to_all | solution.py:239
  49.0 1.0 copy-start.2
  59.3 0.7 copy-start.6
  91.6 14.0 %all-to-all-start.4 = ((f32[8,32,256]{2,1,0:T(8,128)}), f32[8,32,256]{2,1,0:T(8,128)S(1)}, u32[]{:S(2)}, u32[]{:S(2)}) async-start(f32[8,32,256]{2,1,0:T(8,128)} %convolution_bitcast_fusion), calls=%async_computation.4 | async-start | bytes 524288 | tf_op jit(solution)/shard_map/all_to_all | solution.py:239
  119.8 36.9 %all-to-all-start.6 = ((bf16[128,8,128]{2,1,0:T(8,128)(2,1)}), bf16[128,8,128]{2,1,0:T(8,128)(2,1)S(1)}, u32[]{:S(2)}, u32[]{:S(2)}) async-start(bf16[128,8,128]{2,1,0:T(8,128)(2,1)} %broadcast_in_dim.16), calls=%async_computation.6 | async-start | bytes 524288 | tf_op jit(solution)/shard_map/all_to_all | solution.py:239
  148.5 9.6 %collective-permute-start.2 = (bf16[32,256]{1,0:T(8,128)(2,1)S(1)}, bf16[32,256]{1,0:T(8,128)(2,1)S(1)}, u32[]{:S(2)}, u32[]{:S(2)}) collective-permute-start(bf16[32,256]{1,0:T(8,128)(2,1)S(1)} %multiply_convert_fusion), channel_id=1, source_target_pairs={{0,1},{1,0},{2,3},{3,2},{4,5},{5,4},{6,7},{7,6},{8,9},{9,8},{10,11... | collective-permute-start | bytes 49160 | tf_op jit(solution)/shard_map/ppermute | solution.py:253
  156.7 11.7 %collective-permute-start.6 = (bf16[128,8,128]{2,1,0:T(8,128)(2,1)S(1)}, bf16[128,8,128]{2,1,0:T(8,128)(2,1)S(1)}, u32[]{:S(2)}, u32[]{:S(2)}) collective-permute-start(bf16[128,8,128]{2,1,0:T(8,128)(2,1)S(1)} %all-to-all-done.6), channel_id=1, source_target_pairs={{0,8},{8,0},{1,9},{9,1},{2,10},{10,2},{3,11},{11,3},{4,12},{12,4},... | collective-permute-start | bytes 786440 | tf_op jit(solution)/shard_map/ppermute | solution.py:253
  158.1 7.3 %copy-start.7 = (bf16[64,256]{1,0:T(8,128)(2,1)}, bf16[64,256]{1,0:T(8,128)(2,1)S(1)}, u32[]{:S(2)}) copy-start(bf16[64,256]{1,0:T(8,128)(2,1)S(1)} %pad_maximum_fusion.2.refs_0_) | copy-start | bytes 98308
  158.1 6.6 %collective-permute-start.3 = (bf16[64,256]{1,0:T(8,128)(2,1)S(1)}, bf16[64,256]{1,0:T(8,128)(2,1)S(1)}, u32[]{:S(2)}, u32[]{:S(2)}) collective-permute-start(bf16[64,256]{1,0:T(8,128)(2,1)S(1)} %pad_maximum_fusion.2.refs_0_), channel_id=1, source_target_pairs={{0,2},{2,4},{4,6},{6,0},{1,3},{3,5},{5,7},{7,1},{8,10},{10,12},{12... | collective-permute-start | bytes 98312 | tf_op jit(solution)/shard_map/ppermute | solution.py:253
  159.8 4.9 %collective-permute-start.4 = (bf16[64,256]{1,0:T(8,128)(2,1)S(1)}, bf16[64,256]{1,0:T(8,128)(2,1)S(1)}, u32[]{:S(2)}, u32[]{:S(2)}) collective-permute-start(bf16[64,256]{1,0:T(8,128)(2,1)S(1)} %pad_maximum_fusion.2.refs_0_), channel_id=1, source_target_pairs={{0,4},{2,6},{4,0},{6,2},{1,5},{3,7},{5,1},{7,3},{8,12},{10,14},{12... | collective-permute-start | bytes 98312 | tf_op jit(solution)/shard_map/ppermute | solution.py:253
  162.6 2.8 %collective-permute-start.5 = (bf16[64,256]{1,0:T(8,128)(2,1)S(1)}, bf16[64,256]{1,0:T(8,128)(2,1)S(1)}, u32[]{:S(2)}, u32[]{:S(2)}) collective-permute-start(bf16[64,256]{1,0:T(8,128)(2,1)S(1)} %pad_maximum_fusion.2.refs_0_), channel_id=1, source_target_pairs={{0,6},{2,0},{4,2},{6,4},{1,7},{3,1},{5,3},{7,5},{8,14},{10,8},{12,... | collective-permute-start | bytes 98312 | tf_op jit(solution)/shard_map/ppermute | solution.py:253
  164.7 0.7 copy-start.10
  164.7 0.7 copy-start.11
  165.4 0.6 copy-start.12
